TPU v7x, 256 devices: a whole 4x4x8 slice. The times are simulated.
256 devices in a mesh: dp: 8 (over z), expert: 16 (over y, x), tensor: 2 (over core).
Axes of the slice: x: 4, y: 4, z: 8, core: 2. Of those that a mesh axis runs over, the one named last changes fastest.
Arguments:
- tokens: bfloat16 [1536, 7168], P(('dp', 'expert')), may hold values from -6 to 6
- expert_ids: int32 [1536, 8], P(('dp', 'expert')), may hold values from 0 to 15, all different within a row; in each aligned block of 12 rows (0 to 11, 12 to 23, ...) at most 8 rows name the same one
- route_weights: float32 [1536, 8], P(('dp', 'expert')), may hold values from 0.1 to 1
- gate_weights: bfloat16 [16, 7168, 2048], P('expert', 'dp', 'tensor'), may hold values from -0.0625 to 0.0625
- up_weights: bfloat16 [16, 7168, 2048], P('expert', 'dp', 'tensor'), may hold values from -0.0625 to 0.0625
- down_weights: bfloat16 [16, 2048, 7168], P('expert', 'tensor', 'dp'), may hold values from -0.125 to 0.125
- shared_gate: bfloat16 [7168, 2048], P('dp', 'tensor'), may hold values from -0.0625 to 0.0625
- shared_up: bfloat16 [7168, 2048], P('dp', 'tensor'), may hold values from -0.0625 to 0.0625
- shared_down: bfloat16 [2048, 7168], P('tensor', 'dp'), may hold values from -0.125 to 0.125
Outputs:
- mixed: bfloat16 [1536, 7168], P(('dp', 'expert'))
Inputs may be any that keep to these rules, and one draw needn't show every extreme that they name: `expert_ids`: each token names 8 different experts. In the rows of one device no expert is named by more than 8 tokens, and in some device's rows some expert is named by exactly 8.
All inputs are finite; a program needn't handle non-finite values.
Results may differ from a plain program's by a relative error of at most 0.005.
Values may be sent and summed in bfloat16 or wider, within the bound.
No kernel may reach another device: no remote copies, remote signals or barrier semaphores. Data moves between devices by JAX's collectives and lax.ppermute only.
A program may use at most 128 MiB of HBM per device.

v0:
```python
import jax
import jax.numpy as jnp
from jax import lax
from jax.sharding import PartitionSpec as P

EXPERTS = 16
CAP = 8


def in_blocks(x, dim, devices):
    dims = x.shape
    pieces = x.reshape(*dims[:dim], devices, dims[dim] // devices, *dims[dim + 1 :])
    return jnp.moveaxis(pieces, dim, 0)


def in_order(pieces, dim):
    pieces = jnp.moveaxis(pieces, 0, dim)
    dims = pieces.shape
    return pieces.reshape(*dims[:dim], dims[dim] * dims[dim + 1], *dims[dim + 2 :])


def joined_exchange(x, axis, axes, splits, concats):
    sizes = [lax.axis_size(a) for a in axes]
    pieces = in_blocks(x, splits[0], sizes[0])
    pieces = jnp.moveaxis(in_blocks(pieces, splits[1] + 1, sizes[1]), 0, 1)
    inside = pieces.shape[2:]
    pieces = pieces.reshape(-1, *inside)
    pieces = lax.all_to_all(pieces, axis, split_axis=0, concat_axis=0, tiled=True)
    pieces = in_order(pieces.reshape(*sizes, *inside), concats[0] + 1)
    return in_order(pieces, concats[1])


def sum_together(arrays, axis, dims):
    devices = lax.axis_size(axis)
    pieces = [in_blocks(a, dim, devices) for a, dim in zip(arrays, dims)]
    lines = jnp.concatenate([b.reshape(devices, -1) for b in pieces], axis=1)
    width = max(16, -(-lines.shape[1] // 1024) * 8)
    lines = jnp.pad(lines, ((0, 0), (0, width * 128 - lines.shape[1]))).reshape(-1, 128)
    vector, at, done = (lax.psum_scatter(lines, axis, tiled=True).reshape(-1), 0, [])
    for b in pieces:
        part = b[0]
        done.append(vector[at : at + part.size].reshape(part.shape))
        at += part.size
    return tuple(done)


def one_gather(arrays, axis, dims):
    vector = jnp.concatenate([a.reshape(-1) for a in arrays])
    lines, at, done = (lax.all_gather(vector, axis), 0, [])
    for a, dim in zip(arrays, dims):
        pieces = lines[:, at : at + a.size].reshape(-1, *a.shape)
        done.append(in_order(pieces, dim))
        at += a.size
    return tuple(done)


def summed_on_arrival(x, axis, dim):
    pieces = in_blocks(x, dim, lax.axis_size(axis))
    arrived = lax.all_to_all(pieces, axis, split_axis=0, concat_axis=0, tiled=True)
    return arrived.sum(axis=0)


def copy_for_each(x, axis):
    copies = jnp.broadcast_to(x, (lax.axis_size(axis), *x.shape))
    return lax.all_to_all(copies, axis, split_axis=0, concat_axis=0, tiled=True)


def gathered_copies(x, axis, dim):
    return in_order(copy_for_each(x, axis), dim)


def build_slots(block_ids):
    expert_range = jnp.arange(EXPERTS, dtype=jnp.int32)
    marked = (block_ids[:, :, None] == expert_range[None, None, :]).astype(jnp.int32)
    per_token = jnp.sum(marked, axis=1)
    before = jnp.cumsum(per_token, axis=0) - per_token
    position = jnp.sum(marked * before[:, None, :], axis=2)
    return block_ids * CAP + position


def pack_rows(block_tokens, slot_block, slot_count):
    wanted = jnp.arange(slot_count, dtype=jnp.int32)
    picker = jnp.any(wanted[:, None, None] == slot_block[None, :, :], axis=2).astype(jnp.bfloat16)
    return jnp.dot(picker, block_tokens, preferred_element_type=jnp.float32).astype(jnp.bfloat16)


def gated(gate_full, up_full):
    return (jax.nn.silu(gate_full) * up_full).astype(jnp.bfloat16)


def combine_rows(returned, slot_ids, route_weights, shared_part):
    picked = jnp.take(returned, slot_ids, axis=0)
    extra = (1,) * (picked.ndim - 2)
    scaled = route_weights.reshape(route_weights.shape + extra) * picked
    return shared_part + jnp.sum(scaled, axis=1)


def per_device(
    tokens,
    expert_ids,
    route_weights,
    gate_weights,
    up_weights,
    down_weights,
    shared_gate,
    shared_up,
    shared_down,
):
    groups = lax.axis_size("expert")
    dp_count = lax.axis_size("dp")
    token_count = tokens.shape[0]
    model_width = tokens.shape[1]
    local_count = gate_weights.shape[0]
    block_width = gate_weights.shape[1]
    slot_ids = build_slots(expert_ids)
    outgoing = pack_rows(tokens, slot_ids, EXPERTS * CAP).reshape(
        groups, local_count * CAP, dp_count, block_width
    )
    arrived = joined_exchange(outgoing, ("dp", "expert"), ("dp", "expert"), (2, 0), (2, 0))
    own_columns = lax.all_to_all(
        tokens.reshape(token_count, dp_count, block_width),
        "dp",
        split_axis=1,
        concat_axis=1,
        tiled=True,
    )
    grouped = arrived.reshape(groups, local_count, CAP, dp_count, block_width)
    gate_part = jnp.einsum(
        "glcpd,ldf->glcpf", grouped, gate_weights, preferred_element_type=jnp.float32
    )
    up_part = jnp.einsum(
        "glcpd,ldf->glcpf", grouped, up_weights, preferred_element_type=jnp.float32
    )
    shared_gate_part = jnp.einsum(
        "tpd,df->tpf", own_columns, shared_gate, preferred_element_type=jnp.float32
    )
    shared_up_part = jnp.einsum(
        "tpd,df->tpf", own_columns, shared_up, preferred_element_type=jnp.float32
    )
    shared_gate_part = shared_gate_part.reshape(token_count, 1, 1, dp_count, -1)
    shared_up_part = shared_up_part.reshape(token_count, 1, 1, dp_count, -1)
    gate_share, up_share, shared_gate_share, shared_up_share = sum_together(
        (gate_part, up_part, shared_gate_part, shared_up_part), "dp", (3, 3, 3, 3)
    )
    hidden_share = gated(gate_share, up_share)
    shared_share = gated(shared_gate_share, shared_up_share)
    hidden, shared_hidden = one_gather((hidden_share, shared_share), "dp", (3, 3))
    routed_down = jnp.einsum(
        "glcpf,lfd->glcpd", hidden, down_weights, preferred_element_type=jnp.float32
    )
    shared_down_part = jnp.einsum(
        "tabpf,fd->tabpd", shared_hidden, shared_down, preferred_element_type=jnp.float32
    )
    routed_half, shared_half = (
        summed_on_arrival(routed_down, "tensor", 4),
        summed_on_arrival(shared_down_part, "tensor", 4),
    )
    half_width = routed_half.shape[4]
    results = routed_half.reshape(groups, local_count * CAP, dp_count, half_width)
    returned = joined_exchange(results, ("dp", "expert"), ("dp", "expert"), (2, 0), (2, 0)).reshape(
        EXPERTS * CAP, dp_count, half_width
    )
    shared_rows = shared_half.reshape(token_count, dp_count, half_width)
    shared_back = lax.all_to_all(shared_rows, "dp", split_axis=1, concat_axis=1, tiled=True)
    mixed_half = combine_rows(returned, slot_ids, route_weights, shared_back).astype(jnp.bfloat16)
    mixed_rows = gathered_copies(mixed_half, "tensor", 2).reshape(token_count, model_width)
    return mixed_rows


def solution(mesh):
    placed = (
        P(("dp", "expert"), None),
        P(("dp", "expert"), None),
        P(("dp", "expert"), None),
        P("expert", "dp", "tensor"),
        P("expert", "dp", "tensor"),
        P("expert", "tensor", "dp"),
        P("dp", "tensor"),
        P("dp", "tensor"),
        P("tensor", "dp"),
    )
    return jax.shard_map(
        per_device, mesh=mesh, in_specs=placed, out_specs=P(("dp", "expert"), None), check_vma=False
    )
```

profile of v0, /device:TPU:1, one launch (start us, length us, event | category | flops | bytes accessed | tf_op | source)
XLA Modules:
  0.0 390.8 jit_solution(15192280188475355360)
XLA Ops:
  6.5 0.0 copy-start
  6.5 1.1 copy.108
  7.7 0.7 copy.89
  8.4 9.0 %all-to-all-start.1 = ((bf16[12,8,896]{2,0,1:T(8,128)(2,1)}), bf16[12,8,896]{2,0,1:T(8,128)(2,1)S(1)}, u32[]{:S(2)}, u32[]{:S(2)}) async-start(bf16[12,8,896]{2,0,1:T(8,128)(2,1)} %copy.89), calls=%async_computation.1 | async-start | bytes 458752 | tf_op jit(solution)/shard_map/all_to_all | solution.py:120
  17.4 0.8 copy.84
  18.2 0.1 convert_reduce_fusion
  18.3 0.3 select_reduce_fusion
  18.7 0.1 fusion.20
  18.8 0.0 copy-done.5
  18.8 0.7 convolution_convert_fusion
  19.5 1.5 copy.86
  20.9 6.3 %all-to-all-done.1 = bf16[12,8,896]{2,0,1:T(8,128)(2,1)S(1)} async-done(((bf16[12,8,896]{2,0,1:T(8,128)(2,1)}), bf16[12,8,896]{2,0,1:T(8,128)(2,1)S(1)}, u32[]{:S(2)}, u32[]{:S(2)}) %all-to-all-start.1) | async-done | bytes 172064 | tf_op jit(solution)/shard_map/all_to_all | solution.py:120
  27.2 10.4 %all-to-all-start = ((bf16[128,1,8,1,896]{4,2,3,1,0:T(8,128)(2,1)}), bf16[128,1,8,1,896]{4,2,3,1,0:T(8,128)(2,1)}, u32[]{:S(2)}, u32[]{:S(2)}) async-start(bf16[128,1,8,1,896]{4,2,3,1,0:T(8,128)(2,1)} %bitcast.155), calls=%async_computation | async-start | bytes 3670016 | tf_op jit(solution)/shard_map/all_to_all | solution.py:28
  37.6 0.2 reduce-scatter.2.cloned.1.call-start
  37.9 0.0 copy-start.4
  37.9 2.1 fusion.7
  40.0 0.0 copy-done.4
  40.0 0.4 fusion.5
  40.4 40.6 %all-to-all-done = bf16[128,1,8,1,896]{4,2,3,1,0:T(8,128)(2,1)} async-done(((bf16[128,1,8,1,896]{4,2,3,1,0:T(8,128)(2,1)}), bf16[128,1,8,1,896]{4,2,3,1,0:T(8,128)(2,1)}, u32[]{:S(2)}, u32[]{:S(2)}) %all-to-all-start) | async-done | bytes 1835040 | tf_op jit(solution)/shard_map/all_to_all | solution.py:28
  81.1 0.0 copy-done
  81.1 4.1 %fusion.3 = f32[16,8,8,1024]{3,2,1,0:T(8,128)S(1)} fusion(bf16[1,896,1024]{2,1,0:T(8,128)(2,1)S(1)} %copy-done, bf16[8,16,1,8,1,896]{5,3,1,0,4,2:T(8,128)(2,1)} %bitcast.4), kind=kOutput, calls=%fused_computation.8 | convolution fusion | flops 1879048192 | bytes 7864320 | tf_op jit(solution)/shard_map/glcpd,ldf->glcpf/dot_general | solution.py:128
  85.2 0.0 copy-done.7
  85.2 4.0 %fusion.1 = f32[16,8,8,1024]{3,2,1,0:T(8,128)S(1)} fusion(bf16[1,896,1024]{2,1,0:T(8,128)(2,1)S(1)} %copy-done.7, bf16[8,16,1,8,1,896]{5,3,1,0,4,2:T(8,128)(2,1)} %bitcast.4), kind=kOutput, calls=%fused_computation.6 | convolution fusion | flops 1879048192 | bytes 7864320 | tf_op jit(solution)/shard_map/glcpd,ldf->glcpf/dot_general | solution.py:131
  89.2 14.8 %pad_maximum_fusion = f32[8,286720]{1,0:T(8,128)} fusion(f32[8,12288]{1,0:T(8,128)S(1)} %bitcast.162, f32[8,12288]{1,0:T(8,128)S(1)} %bitcast.161, f32[8,131072]{1,0:T(8,128)S(1)} %bitcast.160, f32[8,131072]{1,0:T(8,128)S(1)} %bitcast.159), kind=kLoop, calls=%fused_computation.1 | loop fusion | flops 6881280 | bytes 18350080 | tf_op jit(solution)/shard_map/concatenate | solution.py:36
  104.0 8.5 %reshape.165 = f32[17920,128]{1,0:T(8,128)} reshape(f32[8,286720]{1,0:T(8,128)} %pad_maximum_fusion) | data formatting | bytes 18350080 | tf_op jit(solution)/shard_map/reshape | solution.py:38
  112.5 0.0 reduce-scatter.2.cloned.1.call-update
  112.5 0.0 copy-start.3
  112.5 0.3 all-gather.3.cloned.1.call-start
  112.8 100.1 %reduce-scatter.2.cloned.1.call-done = f32[2240,128]{1,0:T(8,128)} async-done(((f32[17920,128]{1,0:T(8,128)}), f32[2240,128]{1,0:T(8,128)}) %reduce-scatter.2.cloned.1.call-update) | async-done | bytes 1146896 | tf_op jit(solution)/shard_map/reduce_scatter | solution.py:39
  212.9 1.3 fusion.14
  214.2 0.8 fusion.19
  215.1 0.7 pad_maximum_fusion.1
  215.8 0.0 all-gather.3.cloned.1.call-update
  215.8 0.0 copy-done.3
  215.8 2.5 copy.92
  218.3 33.5 %all-gather.3.cloned.1.call-done = bf16[1146880]{0:T(1024)(128)(2,1)} async-done(((bf16[143360]{0:T(1024)(128)(2,1)}), bf16[1146880]{0:T(1024)(128)(2,1)}) %all-gather.3.cloned.1.call-update) | async-done | bytes 2293776 | tf_op jit(solution)/shard_map/all_gather | solution.py:49
  251.8 4.0 %reshape.185 = bf16[8,143360]{1,0:T(8,128)(2,1)} reshape(bf16[1146880]{0:T(1024)(128)(2,1)} %all-gather.3.cloned.1.call-done) | data formatting | bytes 4587520 | tf_op jit(solution)/shard_map/all_gather | solution.py:49
  255.8 1.6 slice-done
  257.4 0.5 copy-done.8
  258.0 4.1 %convolution_bitcast_fusion = f32[16,1,8,8,896]{4,3,2,0,1:T(8,128)} fusion(bf16[16,8,8,1024]{3,2,1,0:T(8,128)(2,1)S(1)} %bitcast.150, bf16[1,1024,896]{2,1,0:T(8,128)(2,1)S(1)} %copy-done.8), kind=kOutput, calls=%fused_computation.4 | convolution fusion | flops 1879048192 | bytes 7602176 | tf_op jit(solution)/shard_map/glcpf,lfd->glcpd/dot_general | solution.py:148
  262.1 7.1 %reshape.175 = f32[16,1,8,8,2,448]{5,4,3,2,0,1:T(2,128)} reshape(f32[16,1,8,8,896]{4,3,2,0,1:T(8,128)} %convolution_bitcast_fusion) | data formatting | bytes 7340032 | tf_op jit(solution)/shard_map/reshape | solution.py:12
  269.2 3.0 copy.125
  272.2 12.1 %all_to_all.35 = f32[2,16,1,8,8,448]{5,4,3,1,2,0:T(8,128)} all-to-all(f32[2,16,1,8,8,448]{5,4,3,1,2,0:T(8,128)S(1)} %bitcast.149), channel_id=1, replica_groups=mesh['dp'=8,'expert'=16,'tensor'=2] {'tensor'}, dimensions={0} | all-to-all | bytes 7340032 | tf_op jit(solution)/shard_map/all_to_all | solution.py:59
  284.4 4.3 %reduce_sum.48 = f32[16,8,8,448]{3,2,1,0:T(8,128)} reduce(f32[2,16,1,8,8,448]{5,4,3,1,2,0:T(8,128)} %all_to_all.35, f32[]{:T(128)} %constant.28.clone.1), dimensions={0,2}, to_apply=%region_6.7 | reduce | flops 458752 | bytes 5505028 | tf_op jit(solution)/shard_map/reduce_sum | solution.py:60
  288.7 4.3 %copy.98 = f32[8,16,8,1,448]{4,2,1,0,3:T(8,128)} copy(f32[8,16,8,1,448]{4,0,2,1,3:T(8,128)} %bitcast.152) | data formatting | bytes 3670016 | tf_op jit(solution)/shard_map/transpose | solution.py:13
  293.0 0.0 slice-done.1
  293.0 0.0 copy-done.2
  293.0 0.7 convolution_bitcast_fusion.1
  293.7 4.0 %all_to_all.36 = f32[2,12,1,1,8,448]{5,4,1,3,2,0:T(8,128)S(1)} all-to-all(f32[2,12,1,1,8,448]{5,4,1,3,2,0:T(8,128)S(1)} %copy.93), channel_id=1, replica_groups=mesh['dp'=8,'expert'=16,'tensor'=2] {'tensor'}, dimensions={0} | all-to-all | bytes 688128 | tf_op jit(solution)/shard_map/all_to_all | solution.py:59
  297.7 12.3 %all-to-all-start.5 = ((f32[128,1,8,1,448]{4,2,3,1,0:T(8,128)}), f32[128,1,8,1,448]{4,2,3,1,0:T(8,128)}, u32[]{:S(2)}, u32[]{:S(2)}) async-start(f32[128,1,8,1,448]{4,2,3,1,0:T(8,128)} %bitcast.153), calls=%async_computation.6 | async-start | bytes 4194304 | tf_op jit(solution)/shard_map/all_to_all | solution.py:28
  310.0 0.1 reshape.179
  310.1 0.1 copy.95
  310.2 0.8 copy.94
  311.1 48.6 %all-to-all-done.5 = f32[128,1,8,1,448]{4,2,3,1,0:T(8,128)} async-done(((f32[128,1,8,1,448]{4,2,3,1,0:T(8,128)}), f32[128,1,8,1,448]{4,2,3,1,0:T(8,128)}, u32[]{:S(2)}, u32[]{:S(2)}) %all-to-all-start.5) | async-done | bytes 1835040 | tf_op jit(solution)/shard_map/all_to_all | solution.py:28
  359.6 4.6 %all-to-all-start.3 = ((f32[12,8,448]{2,0,1:T(8,128)}), f32[12,8,448]{2,0,1:T(8,128)}, u32[]{:S(2)}, u32[]{:S(2)}) async-start(f32[12,8,448]{2,0,1:T(8,128)} %copy.94), calls=%async_computation.4 | async-start | bytes 524288 | tf_op jit(solution)/shard_map/all_to_all | solution.py:164
  364.2 4.6 %copy.100 = f32[8,16,1,8,1,448]{5,0,3,1,4,2:T(8,128)} copy(f32[8,16,1,8,1,448]{5,3,1,0,4,2:T(8,128)} %bitcast.62) | data formatting | bytes 3670016 | tf_op jit(solution)/shard_map/reshape | solution.py:29
  368.7 2.2 gather_fusion
  371.0 0.0 copy-start.1
  371.0 1.0 multiply_reduce_fusion
  372.0 1.8 all-to-all-done.3
  373.7 1.2 fusion.15
  374.9 7.9 %all_to_all.37 = bf16[2,12,8,448]{3,2,1,0:T(8,128)(2,1)S(1)} all-to-all(bf16[2,12,8,448]{3,2,1,0:T(8,128)(2,1)S(1)} %broadcast_in_dim.23), channel_id=1, replica_groups=mesh['dp'=8,'expert'=16,'tensor'=2] {'tensor'}, dimensions={0} | all-to-all | bytes 344064 | tf_op jit(solution)/shard_map/all_to_all | solution.py:65
  382.8 0.2 copy.102
  383.0 1.0 reshape_reshape.27
  (18 shorter events, 0.2 us)
Async XLA Ops:
  6.5 74.5 %copy-start = (bf16[1,896,1024]{2,1,0:T(8,128)(2,1)S(1)}, bf16[1,896,1024]{2,1,0:T(8,128)(2,1)}, u32[]{:S(2)}) copy-start(bf16[1,896,1024]{2,1,0:T(8,128)(2,1)} %param.12) | copy-start | bytes 5505028
  6.5 12.2 %copy-start.5 = (bf16[12,7168]{1,0:T(8,128)(2,1)S(1)}, bf16[12,7168]{1,0:T(8,128)(2,1)}, u32[]{:S(2)}) copy-start(bf16[12,7168]{1,0:T(8,128)(2,1)} %param.9) | copy-start | bytes 516100
  8.4 18.8 %all-to-all-start.1 = ((bf16[12,8,896]{2,0,1:T(8,128)(2,1)}), bf16[12,8,896]{2,0,1:T(8,128)(2,1)S(1)}, u32[]{:S(2)}, u32[]{:S(2)}) async-start(bf16[12,8,896]{2,0,1:T(8,128)(2,1)} %copy.89), calls=%async_computation.1 | async-start | bytes 458752 | tf_op jit(solution)/shard_map/all_to_all | solution.py:120
  27.2 53.9 %all-to-all-start = ((bf16[128,1,8,1,896]{4,2,3,1,0:T(8,128)(2,1)}), bf16[128,1,8,1,896]{4,2,3,1,0:T(8,128)(2,1)}, u32[]{:S(2)}, u32[]{:S(2)}) async-start(bf16[128,1,8,1,896]{4,2,3,1,0:T(8,128)(2,1)} %bitcast.155), calls=%async_computation | async-start | bytes 3670016 | tf_op jit(solution)/shard_map/all_to_all | solution.py:28
  37.6 175.2 %reduce-scatter.2.cloned.1.call-start = ((), (), s32[]{:S(2)}) async-start(), calls=%async_computation.8 | async-start | bytes 10321920 | tf_op jit(solution)/shard_map/reduce_scatter | solution.py:39
  37.9 2.1 copy-start.4
  81.1 4.1 %copy-start.7 = (bf16[1,896,1024]{2,1,0:T(8,128)(2,1)S(1)}, bf16[1,896,1024]{2,1,0:T(8,128)(2,1)}, u32[]{:S(2)}) copy-start(bf16[1,896,1024]{2,1,0:T(8,128)(2,1)} %param.13) | copy-start | bytes 5505028
  112.5 103.3 %copy-start.3 = (bf16[1024,896]{1,0:T(8,128)(2,1)S(1)}, bf16[1024,896]{1,0:T(8,128)(2,1)}, u32[]{:S(2)}) copy-start(bf16[1024,896]{1,0:T(8,128)(2,1)} %param.17) | copy-start | bytes 5505028
  112.5 139.3 %all-gather.3.cloned.1.call-start = ((), (), s32[]{:S(2)}) async-start(), calls=%async_computation.9 | async-start | bytes 2580480 | tf_op jit(solution)/shard_map/all_gather | solution.py:49
  255.8 1.6 slice-start
  255.8 2.1 copy-start.8
  288.7 4.3 %slice-start.1 = ((bf16[8,143360]{1,0:T(8,128)(2,1)}), bf16[8,12288]{1,0:T(8,128)(2,1)S(1)}, s32[]{:S(2)}) async-start(bf16[8,143360]{1,0:T(8,128)(2,1)} %reshape.185), calls=%async_computation.11 | async-start | bytes 393216 | tf_op jit(solution)/shard_map/slice | solution.py:51
  288.7 4.3 %copy-start.2 = (bf16[1024,896]{0,1:T(8,128)(2,1)S(1)}, bf16[1024,896]{0,1:T(8,128)(2,1)}, u32[]{:S(2)}) copy-start(bf16[1024,896]{0,1:T(8,128)(2,1)} %copy.92) | copy-start | bytes 5505028
  297.7 12.4 %copy-start.6 = (f32[12,8]{0,1:T(8,128)S(1)}, f32[12,8]{0,1:T(8,128)}, u32[]{:S(2)}) copy-start(f32[12,8]{0,1:T(8,128)} %param.11) | copy-start | bytes 1156
  297.7 61.9 %all-to-all-start.5 = ((f32[128,1,8,1,448]{4,2,3,1,0:T(8,128)}), f32[128,1,8,1,448]{4,2,3,1,0:T(8,128)}, u32[]{:S(2)}, u32[]{:S(2)}) async-start(f32[128,1,8,1,448]{4,2,3,1,0:T(8,128)} %bitcast.153), calls=%async_computation.6 | async-start | bytes 4194304 | tf_op jit(solution)/shard_map/all_to_all | solution.py:28
  359.6 14.1 %all-to-all-start.3 = ((f32[12,8,448]{2,0,1:T(8,128)}), f32[12,8,448]{2,0,1:T(8,128)}, u32[]{:S(2)}, u32[]{:S(2)}) async-start(f32[12,8,448]{2,0,1:T(8,128)} %copy.94), calls=%async_computation.4 | async-start | bytes 524288 | tf_op jit(solution)/shard_map/all_to_all | solution.py:164
  371.0 13.0 %copy-start.1 = (bf16[1,896,1024]{2,1,0:T(8,128)(2,1)S(1)}, bf16[1,896,1024]{2,1,0:T(8,128)(2,1)}, u32[]{:S(2)}) copy-start(bf16[1,896,1024]{2,1,0:T(8,128)(2,1)} %param.12) | copy-start | bytes 5505028
Sparse Core Ops, SparseCore 0:
  112.6 100.1 reduce-scatter.1
  215.9 35.7 all-gather.2
where the time goes:
time: 392 us; the launch traced here: 391 us
  waiting for transfers between devices  231 us (59%)
  local copies, waits for them, and re-layouts  44.6 us (11%)
  starting transfers between devices  36.7 us (9%)
  other arithmetic  24.8 us (6%)
  blocking collectives  24.1 us (6%)
  matrix products  16.2 us (4%)
  between operations  13.6 us (3%)
    reduce_scatter x1, waiting for transfers between devices, sum_together(): lax.psum_scatter(lines, axis, tiled=True).reshape(-1)  100 us
    all_to_all x2, waiting for transfers between devices, joined_exchange(): lax.all_to_all(pieces, axis, split_axis=0, concat_axis=0, tiled=True)  89.2 us
    all_gather x1, waiting for transfers between devices, one_gather(): lines, at, done = (lax.all_gather(vector, axis), 0, [])  33.5 us
    all_to_all x2, starting transfers between devices, joined_exchange(): lax.all_to_all(pieces, axis, split_axis=0, concat_axis=0, tiled=True)  22.7 us
    all_to_all x2, blocking collectives, summed_on_arrival(): lax.all_to_all(pieces, axis, split_axis=0, concat_axis=0, tiled=True)  16.2 us
    concatenate x1, other arithmetic, sum_together(): lines = jnp.concatenate([b.reshape(devices, -1) for b in pieces], axis=1)  14.8 us
    reshape x2, local copies, waits for them, and re-layouts, in_blocks(): x.reshape(*dims[:dim], devices, dims[dim] // devices, *dims[dim + 1:])  10.1 us
    all_to_all x1, starting transfers between devices, per_device(): lax.all_to_all(tokens.reshape(token_count, dp_count, block_width), 'dp',...  9 us
  transfers between devices with their start and end apart: 6, of which 6 were waited for; matrix products, arithmetic and copies ran while one was open for 4% of the time, Pallas kernels for 0%

commit v1 on v0

v1 whole, which is shorter than its diff:
```python
import functools

import jax
import jax.numpy as jnp
from jax import lax
from jax.experimental import pallas as pl
from jax.experimental.pallas import tpu as pltpu
from jax.sharding import PartitionSpec as P

EXPERTS = 16
CAP = 8
TOP = 8
ZN = 8
TOK = 12
PADT = 16
BLOCK = 896
HALF = 448
WIDE = 512
ROWS = EXPERTS * CAP
CHUNK = ROWS + PADT
FFH = 1024
NT = 256
ORDER = (3, 4, 5, 6, 7, 0, 1, 2)
SCALE = 16.0
LINK = jnp.float16

PARAMS = pltpu.CompilerParams(vmem_limit_bytes=24 * 1024 * 1024)
VMEM = pl.BlockSpec(memory_space=pltpu.VMEM)
SMEM = pl.BlockSpec(memory_space=pltpu.SMEM)
SWAP = [(0, 1), (1, 0)]


def shifted(k):
    return [(i, (i + k) % ZN) for i in range(ZN)]


def paired(up, down):
    out = []
    for i in range(ZN):
        out.append((i * 2, ((i + up) % ZN) * 2))
        out.append((i * 2 + 1, ((i - down) % ZN) * 2 + 1))
    return out


def fdot(a, b):
    return jnp.dot(a, b, preferred_element_type=jnp.float32)


def prep_kernel(c_ref, x_ref, ids_ref, w_ref, out_ref):
    first = c_ref[0] == 0
    w = w_ref[...]
    hi = w.astype(jnp.bfloat16)
    rest = w - hi.astype(jnp.float32)
    mid = rest.astype(jnp.bfloat16)
    low = (rest - mid.astype(jnp.float32)).astype(jnp.bfloat16)
    lane = lax.broadcasted_iota(jnp.int32, (TOP, 128), 1)
    part = lax.broadcasted_iota(jnp.int32, (TOP, 128), 0)
    start = jnp.where(first, 64, 0)
    ext = jnp.zeros((TOK, 128), jnp.float32)
    for i, v in enumerate((ids_ref[...].astype(jnp.float32).astype(jnp.bfloat16), hi, mid, low)):
        ext = ext + fdot(v, (lane == start + TOP * i + part).astype(jnp.bfloat16))
    lanes = lax.broadcasted_iota(jnp.int32, (TOK, 128), 1)
    routing = lanes // 64 == jnp.where(first, 1, 0)
    for b in range(ZN):
        at = b * BLOCK

        @pl.when(first)
        def _():
            out_ref[b, :, :384] = x_ref[:, at : at + 384]
            edge = x_ref[:, at + 384 : at + 512].astype(jnp.float32)
            out_ref[b, :, 384:] = jnp.where(routing, ext, edge).astype(jnp.bfloat16)

        @pl.when(jnp.logical_not(first))
        def _():
            edge = x_ref[:, at + 384 : at + 512].astype(jnp.float32)
            out_ref[b, :, :128] = jnp.where(routing, ext, edge).astype(jnp.bfloat16)
            out_ref[b, :, 128:] = x_ref[:, at + 512 : at + BLOCK]


def prep(c, x, ids, w):
    return pl.pallas_call(
        prep_kernel,
        out_shape=jax.ShapeDtypeStruct((ZN, TOK, WIDE), jnp.bfloat16),
        in_specs=[SMEM, VMEM, VMEM, VMEM],
        out_specs=VMEM,
        compiler_params=PARAMS,
        name="prep",
    )(c, x, ids, w)


def pack_kernel(s_ref, x_ref, packed_ref, shared_ref, ext_ref):
    z = s_ref[0]
    n = ZN * TOK
    x = x_ref[...].astype(jnp.float32)
    x = jnp.where(s_ref[1] == 0, x, pltpu.roll(x, WIDE - 64, 1))
    ext = x[:, WIDE - 128 :]
    ext_ref[...] = ext.astype(jnp.bfloat16)
    x = x.astype(jnp.bfloat16)[:, :HALF]
    ids = jnp.transpose(ext)[64:72, :].astype(jnp.int32)
    experts = lax.broadcasted_iota(jnp.int32, (EXPERTS, n), 0)
    member = jnp.zeros((EXPERTS, n), jnp.float32)
    for k in range(TOP):
        member = member + (experts == ids[k : k + 1, :]).astype(jnp.float32)
    r0 = lax.broadcasted_iota(jnp.int32, (n, n), 0)
    r1 = lax.broadcasted_iota(jnp.int32, (n, n), 1)
    before = ((r0 // TOK == r1 // TOK) & (r0 < r1)).astype(jnp.bfloat16)
    pos = fdot(member.astype(jnp.bfloat16), before).astype(jnp.int32)
    row = lax.broadcasted_iota(jnp.int32, (1, n), 1)
    zs = row // TOK
    place = (z - zs + 13) % ZN
    target = jnp.where(member > 0.5, place * CAP + pos, -1)
    wanted = lax.broadcasted_iota(jnp.int32, (ZN * CAP, n), 0)
    for e in range(EXPERTS):
        pick = (wanted == target[e : e + 1, :]).astype(jnp.bfloat16)
        packed_ref[e] = fdot(pick, x).astype(jnp.bfloat16)
    wide = lax.broadcasted_iota(jnp.int32, (ZN * PADT, n), 0)
    pick = (wide == place * PADT + row - zs * TOK).astype(jnp.bfloat16)
    shared_ref[...] = fdot(pick, x).astype(jnp.bfloat16)


def pack(s, x):
    return pl.pallas_call(
        pack_kernel,
        out_shape=(
            jax.ShapeDtypeStruct((EXPERTS, ZN * CAP, HALF), jnp.bfloat16),
            jax.ShapeDtypeStruct((ZN * PADT, HALF), jnp.bfloat16),
            jax.ShapeDtypeStruct((ZN * TOK, 128), jnp.bfloat16),
        ),
        in_specs=[SMEM, VMEM],
        out_specs=(VMEM, VMEM, VMEM),
        compiler_params=PARAMS,
        name="pack",
    )(s, x)


def up_kernel(first, count, c_ref, own_ref, oth_ref, so_ref, st_ref, wg_ref, wu_ref, sg_ref, su_ref, *out_refs):
    c = c_ref[0]
    mine = pl.ds(pl.multiple_of(c * HALF, 64), HALF)
    other = pl.ds(pl.multiple_of((1 - c) * HALF, 64), HALF)
    own = own_ref[first : first + count].reshape(count * ROWS, HALF)
    oth = oth_ref[first : first + count].reshape(count * ROWS, HALF)
    so = so_ref[first * PADT : (first + count) * PADT]
    st = st_ref[first * PADT : (first + count) * PADT]
    for w_ref, s_ref, o_refs in ((wg_ref, sg_ref, out_refs[:count]), (wu_ref, su_ref, out_refs[count:])):
        full = (fdot(own, w_ref[0, mine, :]) + fdot(oth, w_ref[0, other, :])) * SCALE
        shared = (fdot(so, s_ref[mine, :]) + fdot(st, s_ref[other, :])) * SCALE
        for i in range(count):
            o_refs[i][:ROWS, :] = full[i * ROWS : (i + 1) * ROWS]
            o_refs[i][ROWS:, :] = shared[i * PADT : (i + 1) * PADT]


def up_dots(first, count, c, own, oth, so, st, wg, wu, sg, su):
    whole = lambda *shape: pl.BlockSpec(shape, lambda n: (0,) * len(shape))
    return pl.pallas_call(
        functools.partial(up_kernel, first, count),
        grid=(FFH // NT,),
        out_shape=(jax.ShapeDtypeStruct((CHUNK, FFH), jnp.float32),) * (2 * count),
        in_specs=[
            SMEM,
            whole(ZN, ROWS, HALF),
            whole(ZN, ROWS, HALF),
            whole(ZN * PADT, HALF),
            whole(ZN * PADT, HALF),
            pl.BlockSpec((1, BLOCK, NT), lambda n: (0, 0, n)),
            pl.BlockSpec((1, BLOCK, NT), lambda n: (0, 0, n)),
            pl.BlockSpec((BLOCK, NT), lambda n: (0, n)),
            pl.BlockSpec((BLOCK, NT), lambda n: (0, n)),
        ],
        out_specs=(pl.BlockSpec((CHUNK, NT), lambda n: (0, n)),) * (2 * count),
        compiler_params=PARAMS,
        cost_estimate=pl.CostEstimate(
            flops=2 * 2 * count * CHUNK * BLOCK * FFH, bytes_accessed=4 * BLOCK * FFH * 2, transcendentals=0
        ),
    )(c, own, oth, so, st, wg, wu, sg, su)


def down_kernel(c_ref, *refs):
    xs, (wd_ref, sd_ref, keep_ref, send_ref) = refs[:-4], refs[-4:]
    n = len(xs) // 2
    full = fdot(jnp.concatenate([x[:ROWS] for x in xs], axis=0), wd_ref[0])
    shared = fdot(jnp.concatenate([x[ROWS:] for x in xs], axis=0), sd_ref[...])

    def store(ref, i, at):
        ref[i, :ROWS] = full[at * ROWS : (at + 1) * ROWS]
        ref[i, ROWS:] = shared[at * PADT : (at + 1) * PADT]

    @pl.when(c_ref[0] == 0)
    def _():
        for i in range(n):
            store(keep_ref, i, i)
            store(send_ref, i, n + i)

    @pl.when(c_ref[0] != 0)
    def _():
        for i in range(n):
            store(keep_ref, i, n + i)
            store(send_ref, i, i)


def down_dots(c, xs, wd, sd):
    n = len(xs) // 2
    return pl.pallas_call(
        down_kernel,
        out_shape=(
            jax.ShapeDtypeStruct((n, CHUNK, BLOCK), jnp.float32),
            jax.ShapeDtypeStruct((n, CHUNK, BLOCK), jnp.float32),
        ),
        in_specs=[SMEM] + [VMEM] * (len(xs) + 2),
        out_specs=(VMEM, VMEM),
        compiler_params=PARAMS,
        cost_estimate=pl.CostEstimate(
            flops=2 * 2 * n * CHUNK * BLOCK * FFH, bytes_accessed=2 * BLOCK * FFH * 2, transcendentals=0
        ),
        name="down_dots",
    )(c, *xs, wd, sd)


def combine_kernel(zs_ref, ext_ref, back_ref, shared_ref, out_ref):
    n = ZN * TOK
    rows = 2 * PADT
    cols = 2 * ROWS
    t = lax.broadcasted_iota(jnp.int32, (rows, n), 0)
    r = lax.broadcasted_iota(jnp.int32, (rows, n), 1)
    zs = jnp.where(t < PADT, zs_ref[0], zs_ref[1])
    pick = ((r == zs * TOK + t % PADT) & (t % PADT < TOK)).astype(jnp.bfloat16)
    ext = fdot(pick, ext_ref[...])
    weight = (ext[:, 72:80] + ext[:, 80:88]) + ext[:, 88:96]
    column = lax.broadcasted_iota(jnp.int32, (rows, cols), 1)
    row = lax.broadcasted_iota(jnp.int32, (rows, cols), 0)
    live = (row % PADT < TOK) & (row // PADT == (column // CAP) % 2)
    owner = (column // (2 * CAP)).astype(jnp.float32)
    slot = (column % CAP).astype(jnp.float32)
    member = jnp.zeros((rows, cols), jnp.float32)
    scale = jnp.zeros((rows, cols), jnp.float32)
    for k in range(TOP):
        hit = (ext[:, 64 + k : 65 + k] == owner) & live
        member = jnp.where(hit, 1.0, member)
        scale = jnp.where(hit, weight[:, k : k + 1], scale)
    i0 = lax.broadcasted_iota(jnp.int32, (rows, rows), 0)
    i1 = lax.broadcasted_iota(jnp.int32, (rows, rows), 1)
    before = ((i1 < i0) & (i0 // PADT == i1 // PADT)).astype(jnp.bfloat16)
    pos = fdot(before, member.astype(jnp.bfloat16))
    scale = jnp.where((pos == slot) & (member > 0.5), scale, 0.0)
    hi = scale.astype(jnp.bfloat16)
    rest = scale - hi.astype(jnp.float32)
    mid = rest.astype(jnp.bfloat16)
    low = (rest - mid.astype(jnp.float32)).astype(jnp.bfloat16)
    back = back_ref[...]
    total = (fdot(low, back) + fdot(mid, back)) + fdot(hi, back)
    out_ref[...] = (shared_ref[...] + total).astype(jnp.bfloat16)


def combine(zs, ext, back, shared):
    return pl.pallas_call(
        combine_kernel,
        out_shape=jax.ShapeDtypeStruct((2 * PADT, BLOCK), jnp.bfloat16),
        in_specs=[SMEM, VMEM, VMEM, VMEM],
        out_specs=VMEM,
        compiler_params=PARAMS,
        name="combine",
    )(zs, ext, back, shared)


def assemble_kernel(s_ref, *refs):
    out_ref = refs[-1]
    z = s_ref[0]
    a1, a2, b3, b0, o1, o2, o3, o0 = refs[:-1]

    def put(parts):
        for i, ref in enumerate(parts):
            at = pl.multiple_of(((z + i) % ZN) * BLOCK, 128)
            out_ref[:, pl.ds(at, BLOCK)] = ref[:TOK]

    @pl.when(s_ref[1] == 0)
    def _():
        put((b0, o1, o2, o3, o0, b3, a2, a1))

    @pl.when(s_ref[1] != 0)
    def _():
        put((o0, a1, a2, b3, b0, o3, o2, o1))


def assemble(s, *parts):
    return pl.pallas_call(
        assemble_kernel,
        out_shape=jax.ShapeDtypeStruct((TOK, ZN * BLOCK), jnp.bfloat16),
        in_specs=[SMEM] + [VMEM] * len(parts),
        out_specs=VMEM,
        compiler_params=PARAMS,
        name="assemble",
    )(s, *parts)


def ring(parts, shift):
    total = None
    for mine in parts:
        total = mine if total is None else mine + total.astype(jnp.float32)
        total = lax.ppermute(total.astype(LINK), "dp", shifted(shift))
    return total.astype(jnp.float32)


def layer(tokens, ids, weights, wg, wu, wd, sg, su, sd):
    z = lax.axis_index("dp")
    c = lax.axis_index("tensor")
    c1, zc = c.reshape(1), jnp.stack([z, c])
    pieces = prep(c1, tokens, ids, weights)
    column = lax.all_to_all(pieces, "dp", 0, 0, tiled=True).reshape(ZN * TOK, WIDE)
    packed, shared_own, ext = pack(zc, column)
    shared_oth = lax.ppermute(shared_own, "tensor", SWAP)
    arrived = lax.all_to_all(packed, "expert", 0, 0, tiled=True)
    other = lax.ppermute(arrived, "tensor", SWAP)

    def by_chunk(a):
        a = a.reshape(EXPERTS, ZN, CAP, HALF)
        return jnp.moveaxis(a, 1, 0).reshape(ZN, ROWS, HALF)

    own, oth = by_chunk(arrived), by_chunk(other)
    args = (c1, own, oth, shared_own, shared_oth, wg, wu, sg, su)
    early = up_dots(0, 3, *args)
    late = up_dots(3, 5, *args)
    gate = dict(zip(ORDER, early[:3] + late[:5]))
    up = dict(zip(ORDER, early[3:] + late[5:]))
    g_down = ring([gate[k] for k in (4, 3, 2, 1)], -1)
    u_up = ring([up[k] for k in (4, 5, 6, 7)], 1)
    u_down = ring([up[k] for k in (3, 2, 1)], -1)
    g_up = ring([gate[k] for k in (5, 6, 7)], 1)
    g = (gate[0] + (g_down + g_up)) * (1.0 / SCALE)
    u = (up[0] + (u_down + u_up)) * (1.0 / SCALE)
    hidden = (jax.nn.silu(g) * u).astype(jnp.bfloat16)
    got = {0: hidden}
    down, above = hidden, hidden
    for j in range(1, 4):
        down = lax.ppermute(down, "dp", shifted(-1))
        above = lax.ppermute(above, "dp", shifted(1))
        got[ZN - j], got[j] = down, above
    cut = CHUNK // 2
    down = lax.ppermute(down[:cut], "dp", shifted(-1))
    above = lax.ppermute(above[cut:], "dp", shifted(1))
    got[4] = jnp.concatenate([down, above])
    held = {}
    for a, b, sends in (((7, 6), (1, 2), ((1, 1), (2, 2))), ((5, 0), (3, 4), ((3, 3), (0, 4)))):
        keep, send = down_dots(c1, [got[k] for k in a + b], wd, sd)
        total = keep + lax.ppermute(send, "tensor", SWAP)
        rows = total[:, :ROWS].astype(jnp.bfloat16).reshape(2, EXPERTS, CAP, BLOCK)
        rows = jnp.moveaxis(rows, 0, 1).reshape(EXPERTS, 2 * CAP, BLOCK)
        back = lax.all_to_all(rows, "expert", 0, 0, tiled=True).reshape(2 * ROWS, BLOCK)
        ks = jnp.where(c == 0, jnp.array(a), jnp.array(b))
        shared = total[:, ROWS:].reshape(2 * PADT, BLOCK)
        mixed = combine((z - ks) % ZN, ext, back, shared)
        for i, (to, fro) in enumerate(sends):
            held[to] = lax.ppermute(mixed[i * PADT : (i + 1) * PADT], ("dp", "tensor"), paired(to, fro))
    parts = [held[1], held[2], held[3], held[0]]
    others = []
    for p in parts:
        others.append(lax.ppermute(p, "tensor", SWAP))
    return assemble(zc, *parts, *others)


def solution(mesh):
    placed = (
        P(("dp", "expert"), None),
        P(("dp", "expert"), None),
        P(("dp", "expert"), None),
        P("expert", "dp", "tensor"),
        P("expert", "dp", "tensor"),
        P("expert", "tensor", "dp"),
        P("dp", "tensor"),
        P("dp", "tensor"),
        P("tensor", "dp"),
    )
    return jax.shard_map(
        layer, mesh=mesh, in_specs=placed, out_specs=P(("dp", "expert"), None), check_vma=False
    )
```

time: 392 us -> 188 us (0.48)
  waiting for transfers between devices: 231 us -> 58 us
  starting transfers between devices: 36.7 us -> 76.1 us
  local copies, waits for them, and re-layouts: 44.6 us -> 7.86 us
  other arithmetic: 24.8 us -> 4.16 us
  Pallas kernels: 0 us -> 19.6 us
  matrix products: 16.2 us -> 0 us
  between operations: 13.6 us -> 0.44 us
    reduce_scatter x1 -> x0, waiting for transfers between devices: 100 us -> none  [sum_together(): lax.psum_scatter(lines, axis, tiled=True).reshape(-1)]
    all_to_all x4 -> x3, waiting for transfers between devices: 97.2 us -> 19.9 us  [the longest x2 12.3 us: layer(): lax.all_to_all(rows, 'expert', 0, 0, tiled=True).reshape(2 * ROWS, BLOCK)]
    ppermute x0 -> x34, starting transfers between devices: none -> 59.9 us  [the longest x14 23.2 us: ring(): total = lax.ppermute(total.astype(LINK), 'dp', shifted(shift))]
    ppermute x0 -> x34, waiting for transfers between devices: none -> 38 us  [the longest x14 18.9 us: ring(): total = lax.ppermute(total.astype(LINK), 'dp', shifted(shift))]
    all_gather x1 -> x0, waiting for transfers between devices: 33.5 us -> none  [one_gather(): lines, at, done = (lax.all_gather(vector, axis), 0, [])]
    reshape x6 -> x5, local copies, waits for them, and re-layouts: 23.9 us -> 1.85 us  [the longest x2 1.66 us: layer(): rows = jnp.moveaxis(rows, 0, 1).reshape(EXPERTS, 2 * CAP, BLOCK)]
    all_to_all x4 -> x3, starting transfers between devices: 36.3 us -> 16.1 us  [the longest x1 9 us: layer(): lax.all_to_all(pieces, 'dp', 0, 0, tiled=True).reshape(ZN * TOK, WIDE)]
    pallas_call x0 -> x9, Pallas kernels: none -> 19.6 us  [the longest x2 9.55 us: up_dots(): pl.pallas_call(functools.partial(up_kernel, first, count), grid=(FFH // N...]
  transfers between devices with their start and end apart: 6 -> 37, of which waited for: 6 -> 19; matrix products, arithmetic and copies ran while one was open for 4% -> 3% of each run, Pallas kernels for 0% -> 6%
where the time goes in v1:
time: 188 us
  starting transfers between devices  76.1 us (40%)
  waiting for transfers between devices  58 us (31%)
  blocking collectives  21.6 us (11%)
  Pallas kernels  19.6 us (10%)
  local copies, waits for them, and re-layouts  7.86 us (4%)
  other arithmetic  4.16 us (2%)
    ppermute x14, starting transfers between devices, ring(): total = lax.ppermute(total.astype(LINK), 'dp', shifted(shift))  23.2 us
    all_to_all x1, blocking collectives, layer(): arrived = lax.all_to_all(packed, 'expert', 0, 0, tiled=True)  21.6 us
    ppermute x14, waiting for transfers between devices, ring(): total = lax.ppermute(total.astype(LINK), 'dp', shifted(shift))  18.9 us
    ppermute x2, starting transfers between devices, layer(): total = keep + lax.ppermute(send, 'tensor', SWAP)  12.4 us
    all_to_all x2, waiting for transfers between devices, layer(): lax.all_to_all(rows, 'expert', 0, 0, tiled=True).reshape(2 * ROWS, BLOCK)  12.3 us
    pallas_call x2, Pallas kernels, up_dots(): pl.pallas_call(functools.partial(up_kernel, first, count), grid=(FFH // N...  9.55 us
    ppermute x3, starting transfers between devices, layer(): down = lax.ppermute(down, 'dp', shifted(-1))  9.19 us
    all_to_all x1, starting transfers between devices, layer(): lax.all_to_all(pieces, 'dp', 0, 0, tiled=True).reshape(ZN * TOK, WIDE)  9 us
  transfers between devices with their start and end apart: 37, of which 19 were waited for; matrix products, arithmetic and copies ran while one was open for 3% of the time, Pallas kernels for 6%

profile of v1, /device:TPU:1, one launch (start us, length us, event | category | flops | bytes accessed | tf_op | source)
XLA Modules:
  0.0 187.7 jit_solution(2929189186270651996)
XLA Ops:
  0.0 0.8 copy.20.ids_ref
  0.8 0.8 copy.21.w_ref
  1.5 0.9 copy-done.7
  2.5 0.8 prep.1
  3.3 9.0 %all-to-all-start = ((bf16[8,12,512]{2,1,0:T(8,128)(2,1)}), bf16[8,12,512]{2,1,0:T(8,128)(2,1)S(1)}, u32[]{:S(2)}, u32[]{:S(2)}) async-start(bf16[8,12,512]{2,1,0:T(8,128)(2,1)} %prep.1), calls=%async_computation | async-start | bytes 262144 | tf_op jit(solution)/shard_map/all_to_all | solution.py:307
  12.4 7.7 %all-to-all-done = bf16[8,12,512]{2,1,0:T(8,128)(2,1)S(1)} async-done(((bf16[8,12,512]{2,1,0:T(8,128)(2,1)}), bf16[8,12,512]{2,1,0:T(8,128)(2,1)S(1)}, u32[]{:S(2)}, u32[]{:S(2)}) %all-to-all-start) | async-done | bytes 98336 | tf_op jit(solution)/shard_map/all_to_all | solution.py:307
  20.1 1.3 pack.1
  21.4 21.6 %all_to_all.20 = bf16[16,64,448]{2,1,0:T(8,128)(2,1)S(1)} all-to-all(bf16[16,64,448]{2,1,0:T(8,128)(2,1)S(1)} %get-tuple-element.29), channel_id=1, replica_groups=mesh['dp'=8,'expert'=16,'tensor'=2] {'expert'}, dimensions={0} | all-to-all | bytes 1835008 | tf_op jit(solution)/shard_map/all_to_all | solution.py:310
  43.0 3.3 %collective-permute-start = (bf16[16,64,448]{2,1,0:T(8,128)(2,1)S(1)}, bf16[16,64,448]{2,1,0:T(8,128)(2,1)S(1)}, u32[]{:S(2)}, u32[]{:S(2)}) collective-permute-start(bf16[16,64,448]{2,1,0:T(8,128)(2,1)S(1)} %all_to_all.20), channel_id=1, source_target_pairs={{0,1},{1,0},{2,3},{3,2},{4,5},{5,4},{6,7},{7,6},{8,9},{9,8},{10,11... | collective-permute-start | bytes 2752520 | tf_op jit(solution)/shard_map/ppermute | solution.py:311
  46.5 2.1 %collective-permute-done = bf16[16,64,448]{2,1,0:T(8,128)(2,1)S(1)} collective-permute-done((bf16[16,64,448]{2,1,0:T(8,128)(2,1)S(1)}, bf16[16,64,448]{2,1,0:T(8,128)(2,1)S(1)}, u32[]{:S(2)}, u32[]{:S(2)}) %collective-permute-start) | collective-permute-done | bytes 917536 | tf_op jit(solution)/shard_map/ppermute | solution.py:311
  48.8 1.5 copy-done.5
  50.3 4.1 %shard_map.128 = (f32[144,1024]{1,0:T(8,128)S(1)}, f32[144,1024]{1,0:T(8,128)S(1)}, f32[144,1024]{1,0:T(8,128)S(1)}, f32[144,1024]{1,0:T(8,128)S(1)}, f32[144,1024]{1,0:T(8,128)S(1)}, /*index=5*/f32[144,1024]{1,0:T(8,128)S(1)}) custom-call(s32[1]{0:T(128)} %bitcast.1.c_ref, bf16[8,128,448]{2,1,0:T(8,128)(2,1)S(1)} %copy_bitcast_fusion.1.own_ref, ...), custom_call_target="tpu_custom_call" | custom-call | flops 1585446912 | bytes 7340032 | tf_op jit(solution)/shard_map/pallas_call | solution.py:154
  54.5 0.7 collective-permute-start.12
  55.3 2.1 %collective-permute-start.9 = (f16[144,1024]{1,0:T(8,128)(2,1)S(1)}, f16[144,1024]{1,0:T(8,128)(2,1)S(1)}, u32[]{:S(2)}, u32[]{:S(2)}) collective-permute-start(f16[144,1024]{1,0:T(8,128)(2,1)S(1)} %convert_element_type.103), channel_id=1, source_target_pairs={{0,224},{32,0},{64,32},{96,64},{128,96},{160,128},{192,160},{224,1... | collective-permute-start | bytes 884744 | tf_op jit(solution)/shard_map/ppermute | solution.py:298
  57.4 2.7 %collective-permute-start.2 = (f16[144,1024]{1,0:T(8,128)(2,1)S(1)}, f16[144,1024]{1,0:T(8,128)(2,1)S(1)}, u32[]{:S(2)}, u32[]{:S(2)}) collective-permute-start(f16[144,1024]{1,0:T(8,128)(2,1)S(1)} %convert_element_type.89), channel_id=1, source_target_pairs={{0,224},{32,0},{64,32},{96,64},{128,96},{160,128},{192,160},{224,1... | collective-permute-start | bytes 884744 | tf_op jit(solution)/shard_map/ppermute | solution.py:298
  60.1 5.4 %shard_map.127 = (f32[144,1024]{1,0:T(8,128)S(1)}, f32[144,1024]{1,0:T(8,128)S(1)}, f32[144,1024]{1,0:T(8,128)S(1)}, f32[144,1024]{1,0:T(8,128)S(1)}, f32[144,10...) custom-call(s32[1]{0:T(128)} %bitcast.1.c_ref, ...), custom_call_target="tpu_custom_call" | custom-call | flops 2642411520 | bytes 7340032 | tf_op jit(solution)/shard_map/pallas_call | solution.py:154
  65.7 3.9 %collective-permute-done.2 = f16[144,1024]{1,0:T(8,128)(2,1)S(1)} collective-permute-done((f16[144,1024]{1,0:T(8,128)(2,1)S(1)}, f16[144,1024]{1,0:T(8,128)(2,1)S(1)}, u32[]{:S(2)}, u32[]{:S(2)}) %collective-permute-start.2) | collective-permute-done | bytes 294944 | tf_op jit(solution)/shard_map/ppermute | solution.py:298
  69.7 3.3 %collective-permute-start.3 = (f16[144,1024]{1,0:T(8,128)(2,1)S(1)}, f16[144,1024]{1,0:T(8,128)(2,1)S(1)}, u32[]{:S(2)}, u32[]{:S(2)}) collective-permute-start(f16[144,1024]{1,0:T(8,128)(2,1)S(1)} %add_convert_fusion.9), channel_id=1, source_target_pairs={{0,224},{32,0},{64,32},{96,64},{128,96},{160,128},{192,160},{224,1... | collective-permute-start | bytes 884744 | tf_op jit(solution)/shard_map/ppermute | solution.py:298
  73.3 2.7 %collective-permute-start.10 = (f16[144,1024]{1,0:T(8,128)(2,1)S(1)}, f16[144,1024]{1,0:T(8,128)(2,1)S(1)}, u32[]{:S(2)}, u32[]{:S(2)}) collective-permute-start(f16[144,1024]{1,0:T(8,128)(2,1)S(1)} %add_convert_fusion.4), channel_id=1, source_target_pairs={{0,224},{32,0},{64,32},{96,64},{128,96},{160,128},{192,160},{224,1... | collective-permute-start | bytes 884744 | tf_op jit(solution)/shard_map/ppermute | solution.py:298
  76.0 1.8 collective-permute-done.3
  78.0 3.5 %collective-permute-start.4 = (f16[144,1024]{1,0:T(8,128)(2,1)S(1)}, f16[144,1024]{1,0:T(8,128)(2,1)S(1)}, u32[]{:S(2)}, u32[]{:S(2)}) collective-permute-start(f16[144,1024]{1,0:T(8,128)(2,1)S(1)} %add_convert_fusion.8), channel_id=1, source_target_pairs={{0,224},{32,0},{64,32},{96,64},{128,96},{160,128},{192,160},{224,1... | collective-permute-start | bytes 884744 | tf_op jit(solution)/shard_map/ppermute | solution.py:298
  81.5 0.3 collective-permute-done.7
  81.9 0.6 collective-permute-start.8
  82.6 0.4 collective-permute-start.14
  82.9 1.3 collective-permute-done.10
  84.3 3.5 %collective-permute-start.11 = (f16[144,1024]{1,0:T(8,128)(2,1)S(1)}, f16[144,1024]{1,0:T(8,128)(2,1)S(1)}, u32[]{:S(2)}, u32[]{:S(2)}) collective-permute-start(f16[144,1024]{1,0:T(8,128)(2,1)S(1)} %add_convert_fusion.3), channel_id=1, source_target_pairs={{0,224},{32,0},{64,32},{96,64},{128,96},{160,128},{192,160},{224,1... | collective-permute-start | bytes 884744 | tf_op jit(solution)/shard_map/ppermute | solution.py:298
  87.8 2.7 %collective-permute-done.4 = f16[144,1024]{1,0:T(8,128)(2,1)S(1)} collective-permute-done((f16[144,1024]{1,0:T(8,128)(2,1)S(1)}, f16[144,1024]{1,0:T(8,128)(2,1)S(1)}, u32[]{:S(2)}, u32[]{:S(2)}) %collective-permute-start.4) | collective-permute-done | bytes 294944 | tf_op jit(solution)/shard_map/ppermute | solution.py:298
  90.6 3.5 %collective-permute-start.5 = (f16[144,1024]{1,0:T(8,128)(2,1)S(1)}, f16[144,1024]{1,0:T(8,128)(2,1)S(1)}, u32[]{:S(2)}, u32[]{:S(2)}) collective-permute-start(f16[144,1024]{1,0:T(8,128)(2,1)S(1)} %add_convert_fusion.7), channel_id=1, source_target_pairs={{0,224},{32,0},{64,32},{96,64},{128,96},{160,128},{192,160},{224,1... | collective-permute-start | bytes 884744 | tf_op jit(solution)/shard_map/ppermute | solution.py:298
  94.3 2.5 %collective-permute-done.11 = f16[144,1024]{1,0:T(8,128)(2,1)S(1)} collective-permute-done((f16[144,1024]{1,0:T(8,128)(2,1)S(1)}, f16[144,1024]{1,0:T(8,128)(2,1)S(1)}, u32[]{:S(2)}, u32[]{:S(2)}) %collective-permute-start.11) | collective-permute-done | bytes 294944 | tf_op jit(solution)/shard_map/ppermute | solution.py:298
  96.8 6.3 %collective-permute-done.5 = f16[144,1024]{1,0:T(8,128)(2,1)S(1)} collective-permute-done((f16[144,1024]{1,0:T(8,128)(2,1)S(1)}, f16[144,1024]{1,0:T(8,128)(2,1)S(1)}, u32[]{:S(2)}, u32[]{:S(2)}) %collective-permute-start.5) | collective-permute-done | bytes 294944 | tf_op jit(solution)/shard_map/ppermute | solution.py:298
  103.2 0.4 multiply_convert_fusion.refs_1_
  103.6 3.5 %collective-permute-start.16 = (bf16[144,1024]{1,0:T(8,128)(2,1)S(1)}, bf16[144,1024]{1,0:T(8,128)(2,1)S(1)}, u32[]{:S(2)}, u32[]{:S(2)}) collective-permute-start(bf16[144,1024]{1,0:T(8,128)(2,1)S(1)} %multiply_convert_fusion.refs_1_), channel_id=1, source_target_pairs={{0,224},{32,0},{64,32},{96,64},{128,96},{160,128},{192,160},{224,1... | collective-permute-start | bytes 884744 | tf_op jit(solution)/shard_map/ppermute | solution.py:333
  107.1 4.0 %collective-permute-done.18.refs_2_ = bf16[144,1024]{1,0:T(8,128)(2,1)S(1)} collective-permute-done((bf16[144,1024]{1,0:T(8,128)(2,1)S(1)}, bf16[144,1024]{1,0:T(8,128)(2,1)S(1)}, u32[]{:S(2)}, u32[]{:S(2)}) %collective-permute-start.18) | collective-permute-done | bytes 294944 | tf_op jit(solution)/shard_map/ppermute | solution.py:334
  111.1 2.8 %collective-permute-start.17 = (bf16[144,1024]{1,0:T(8,128)(2,1)S(1)}, bf16[144,1024]{1,0:T(8,128)(2,1)S(1)}, u32[]{:S(2)}, u32[]{:S(2)}) collective-permute-start(bf16[144,1024]{1,0:T(8,128)(2,1)S(1)} %collective-permute-done.16.refs_0_), channel_id=1, source_target_pairs={{0,224},{32,0},{64,32},{96,64},{128,96},{160,128},{192,160},{224,1... | collective-permute-start | bytes 884744 | tf_op jit(solution)/shard_map/ppermute | solution.py:333
  113.9 4.6 %collective-permute-done.19.refs_3_ = bf16[144,1024]{1,0:T(8,128)(2,1)S(1)} collective-permute-done((bf16[144,1024]{1,0:T(8,128)(2,1)S(1)}, bf16[144,1024]{1,0:T(8,128)(2,1)S(1)}, u32[]{:S(2)}, u32[]{:S(2)}) %collective-permute-start.19) | collective-permute-done | bytes 294944 | tf_op jit(solution)/shard_map/ppermute | solution.py:334
  118.5 3.0 %collective-permute-start.23 = (bf16[144,1024]{1,0:T(8,128)(2,1)S(1)}, bf16[144,1024]{1,0:T(8,128)(2,1)S(1)}, u32[]{:S(2)}, u32[]{:S(2)}) collective-permute-start(bf16[144,1024]{1,0:T(8,128)(2,1)S(1)} %collective-permute-done.17.refs_1_), channel_id=1, source_target_pairs={{0,224},{32,0},{64,32},{96,64},{128,96},{160,128},{192,160},{224,1... | collective-permute-start | bytes 884744 | tf_op jit(solution)/shard_map/ppermute | solution.py:333
  121.5 1.7 down_dots.2
  123.1 8.5 %collective-permute-start.20 = (f32[2,144,896]{2,1,0:T(8,128)S(1)}, f32[2,144,896]{2,1,0:T(8,128)}, u32[]{:S(2)}, u32[]{:S(2)}) collective-permute-start(f32[2,144,896]{2,1,0:T(8,128)S(1)} %get-tuple-element.48), channel_id=1, source_target_pairs={{0,1},{1,0},{2,3},{3,2},{4,5},{5,4},{6,7},{7,6},{8,9},{9,8},{10,11... | collective-permute-start | bytes 3096584 | tf_op jit(solution)/shard_map/ppermute | solution.py:343
  131.8 2.9 %collective-permute-start.25 = (bf16[72,1024]{1,0:T(8,128)(2,1)S(1)}, bf16[72,1024]{1,0:T(8,128)(2,1)S(1)}, u32[]{:S(2)}, u32[]{:S(2)}) collective-permute-start(bf16[72,1024]{1,0:T(8,128)(2,1)S(1)} %slice.46), channel_id=1, source_target_pairs={{0,224},{32,0},{64,32},{96,64},{128,96},{160,128},{192,160},{224,1... | collective-permute-start | bytes 442376 | tf_op jit(solution)/shard_map/ppermute | solution.py:337
  134.7 2.2 %collective-permute-done.26 = bf16[72,1024]{1,0:T(8,128)(2,1)S(1)} collective-permute-done((bf16[72,1024]{1,0:T(8,128)(2,1)S(1)}, bf16[72,1024]{1,0:T(8,128)(2,1)S(1)}, u32[]{:S(2)}, u32[]{:S(2)}) %collective-permute-start.26) | collective-permute-done | bytes 147488 | tf_op jit(solution)/shard_map/ppermute | solution.py:338
  137.0 2.6 %down_dots.3 = (f32[2,144,896]{2,1,0:T(8,128)S(1)}, f32[2,144,896]{2,1,0:T(8,128)}) custom-call(s32[1]{0:T(128)} %bitcast.1.c_ref, bf16[144,1024]{1,0:T(8,128)(2,1)S(1)} %collective-permute-done.23.refs_0_, bf16[144,1024]{1,0:T(8,128)(2,1)S(1)} %multiply_convert_fusion.refs_1_, bf16[144,1024]{1,0:T(8,128)(2,1)S(1)} %collective-permute-done.24.refs_2_, ...), custom_call_target="tpu_custom_call" | custom-call | flops 1056964608 | bytes 3670016 | tf_op jit(solution)/shard_map/down_dots/pallas_call | solution.py:202
  139.6 3.9 %collective-permute-start.27 = (f32[2,144,896]{2,1,0:T(8,128)}, f32[2,144,896]{2,1,0:T(8,128)}, u32[]{:S(2)}, u32[]{:S(2)}) collective-permute-start(f32[2,144,896]{2,1,0:T(8,128)} %get-tuple-element.50), channel_id=1, source_target_pairs={{0,1},{1,0},{2,3},{3,2},{4,5},{5,4},{6,7},{7,6},{8,9},{9,8},{10,11... | collective-permute-start | bytes 3096584 | tf_op jit(solution)/shard_map/ppermute | solution.py:343
  143.5 1.4 add.78
  144.8 1.0 copy-done.8
  145.9 0.8 copy_bitcast_fusion.3
  146.7 3.6 %all-to-all-start.2 = ((bf16[16,16,896]{2,1,0:T(8,128)(2,1)}), bf16[16,16,896]{2,1,0:T(8,128)(2,1)S(1)}, u32[]{:S(2)}, u32[]{:S(2)}) async-start(bf16[16,16,896]{2,1,0:T(8,128)(2,1)} %copy_bitcast_fusion.3), calls=%async_computation.2 | async-start | bytes 917504 | tf_op jit(solution)/shard_map/all_to_all | solution.py:346
  150.3 1.3 add.80
  151.7 0.8 copy_bitcast_fusion.2
  152.5 8.3 %all-to-all-done.2 = bf16[16,16,896]{2,1,0:T(8,128)(2,1)S(1)} async-done(((bf16[16,16,896]{2,1,0:T(8,128)(2,1)}), bf16[16,16,896]{2,1,0:T(8,128)(2,1)S(1)}, u32[]{:S(2)}, u32[]{:S(2)}) %all-to-all-start.2) | async-done | bytes 458784 | tf_op jit(solution)/shard_map/all_to_all | solution.py:346
  160.8 3.6 %all-to-all-start.3 = ((bf16[16,16,896]{2,1,0:T(8,128)(2,1)}), bf16[16,16,896]{2,1,0:T(8,128)(2,1)S(1)}, u32[]{:S(2)}, u32[]{:S(2)}) async-start(bf16[16,16,896]{2,1,0:T(8,128)(2,1)} %copy_bitcast_fusion.2), calls=%async_computation.3 | async-start | bytes 917504 | tf_op jit(solution)/shard_map/all_to_all | solution.py:346
  164.5 0.9 slice.43
  165.4 1.2 combine.2
  166.6 1.7 collective-permute-start.22
  168.3 1.9 collective-permute-start.21
  170.2 3.9 %all-to-all-done.3 = bf16[16,16,896]{2,1,0:T(8,128)(2,1)S(1)} async-done(((bf16[16,16,896]{2,1,0:T(8,128)(2,1)}), bf16[16,16,896]{2,1,0:T(8,128)(2,1)S(1)}, u32[]{:S(2)}, u32[]{:S(2)}) %all-to-all-start.3) | async-done | bytes 458784 | tf_op jit(solution)/shard_map/all_to_all | solution.py:346
  174.1 1.2 combine.3
  175.3 2.8 %collective-permute-start.29 = (bf16[16,896]{1,0:T(8,128)(2,1)S(1)}, bf16[16,896]{1,0:T(8,128)(2,1)S(1)}, u32[]{:S(2)}, u32[]{:S(2)}) collective-permute-start(bf16[16,896]{1,0:T(8,128)(2,1)S(1)} %get-tuple-element.51), channel_id=1, source_target_pairs={{0,0},{1,129},{32,32},{33,161},{64,64},{65,193},{96,96},{97,225},{... | collective-permute-start | bytes 86024 | tf_op jit(solution)/shard_map/ppermute | solution.py:351
  178.1 1.7 collective-permute-start.28
  179.9 0.4 collective-permute-start.31
  180.4 3.8 %collective-permute-done.29.refs_3_ = bf16[16,896]{1,0:T(8,128)(2,1)S(1)} collective-permute-done((bf16[16,896]{1,0:T(8,128)(2,1)S(1)}, bf16[16,896]{1,0:T(8,128)(2,1)S(1)}, u32[]{:S(2)}, u32[]{:S(2)}) %collective-permute-start.29) | collective-permute-done | bytes 28704 | tf_op jit(solution)/shard_map/ppermute | solution.py:351
  184.2 1.0 collective-permute-done.28.refs_2_
  185.2 0.1 collective-permute-done.33.refs_7_
  185.4 1.0 collective-permute-done.32.refs_6_
  186.4 1.3 assemble.1
  (80 shorter events, 2.2 us)
Async XLA Ops:
  1.5 0.9 copy-start.7
  3.3 16.8 %all-to-all-start = ((bf16[8,12,512]{2,1,0:T(8,128)(2,1)}), bf16[8,12,512]{2,1,0:T(8,128)(2,1)S(1)}, u32[]{:S(2)}, u32[]{:S(2)}) async-start(bf16[8,12,512]{2,1,0:T(8,128)(2,1)} %prep.1), calls=%async_computation | async-start | bytes 262144 | tf_op jit(solution)/shard_map/all_to_all | solution.py:307
  21.4 27.4 %copy-start.4 = (bf16[896,1024]{1,0:T(8,128)(2,1)S(1)}, bf16[896,1024]{1,0:T(8,128)(2,1)}, u32[]{:S(2)}) copy-start(bf16[896,1024]{1,0:T(8,128)(2,1)} %sg_ref.3) | copy-start | bytes 5505028
  43.0 5.6 %collective-permute-start = (bf16[16,64,448]{2,1,0:T(8,128)(2,1)S(1)}, bf16[16,64,448]{2,1,0:T(8,128)(2,1)S(1)}, u32[]{:S(2)}, u32[]{:S(2)}) collective-permute-start(bf16[16,64,448]{2,1,0:T(8,128)(2,1)S(1)} %all_to_all.20), channel_id=1, source_target_pairs={{0,1},{1,0},{2,3},{3,2},{4,5},{5,4},{6,7},{7,6},{8,9},{9,8},{10,11... | collective-permute-start | bytes 2752520 | tf_op jit(solution)/shard_map/ppermute | solution.py:311
  46.3 2.5 %copy-start.2 = (bf16[1,896,1024]{2,1,0:T(8,128)(2,1)S(1)}, bf16[1,896,1024]{2,1,0:T(8,128)(2,1)}, u32[]{:S(2)}) copy-start(bf16[1,896,1024]{2,1,0:T(8,128)(2,1)} %wg_ref.3) | copy-start | bytes 5505028
  46.3 2.5 %copy-start.3 = (bf16[1,896,1024]{2,1,0:T(8,128)(2,1)S(1)}, bf16[1,896,1024]{2,1,0:T(8,128)(2,1)}, u32[]{:S(2)}) copy-start(bf16[1,896,1024]{2,1,0:T(8,128)(2,1)} %wu_ref.3) | copy-start | bytes 5505028
  46.3 2.5 %collective-permute-start.1 = (bf16[128,448]{1,0:T(8,128)(2,1)S(1)}, bf16[128,448]{1,0:T(8,128)(2,1)S(1)}, u32[]{:S(2)}, u32[]{:S(2)}) collective-permute-start(bf16[128,448]{1,0:T(8,128)(2,1)S(1)} %get-tuple-element.30.so_ref), channel_id=1, source_target_pairs={{0,1},{1,0},{2,3},{3,2},{4,5},{5,4},{6,7},{7,6},{8,9},{9,8},{10,11... | collective-permute-start | bytes 344072 | tf_op jit(solution)/shard_map/ppermute | solution.py:309
  48.8 1.5 copy-start.5
  54.4 5.7 %copy-start.6 = (bf16[896,1024]{1,0:T(8,128)(2,1)S(1)}, bf16[896,1024]{1,0:T(8,128)(2,1)}, u32[]{:S(2)}) copy-start(bf16[896,1024]{1,0:T(8,128)(2,1)} %su_ref.3) | copy-start | bytes 5505028
  54.5 11.1 %collective-permute-start.12 = (f16[144,1024]{1,0:T(8,128)(2,1)S(1)}, f16[144,1024]{1,0:T(8,128)(2,1)S(1)}, u32[]{:S(2)}, u32[]{:S(2)}) collective-permute-start(f16[144,1024]{1,0:T(8,128)(2,1)S(1)} %convert_element_type.109), channel_id=1, source_target_pairs={{0,32},{32,64},{64,96},{96,128},{128,160},{160,192},{192,224},{224... | collective-permute-start | bytes 884744 | tf_op jit(solution)/shard_map/ppermute | solution.py:298
  55.3 17.9 %collective-permute-start.9 = (f16[144,1024]{1,0:T(8,128)(2,1)S(1)}, f16[144,1024]{1,0:T(8,128)(2,1)S(1)}, u32[]{:S(2)}, u32[]{:S(2)}) collective-permute-start(f16[144,1024]{1,0:T(8,128)(2,1)S(1)} %convert_element_type.103), channel_id=1, source_target_pairs={{0,224},{32,0},{64,32},{96,64},{128,96},{160,128},{192,160},{224,1... | collective-permute-start | bytes 884744 | tf_op jit(solution)/shard_map/ppermute | solution.py:298
  57.4 15.6 %collective-permute-start.6 = (f16[144,1024]{1,0:T(8,128)(2,1)S(1)}, f16[144,1024]{1,0:T(8,128)(2,1)S(1)}, u32[]{:S(2)}, u32[]{:S(2)}) collective-permute-start(f16[144,1024]{1,0:T(8,128)(2,1)S(1)} %convert_element_type.97), channel_id=1, source_target_pairs={{0,32},{32,64},{64,96},{96,128},{128,160},{160,192},{192,224},{224... | collective-permute-start | bytes 884744 | tf_op jit(solution)/shard_map/ppermute | solution.py:298
  57.4 12.2 %collective-permute-start.2 = (f16[144,1024]{1,0:T(8,128)(2,1)S(1)}, f16[144,1024]{1,0:T(8,128)(2,1)S(1)}, u32[]{:S(2)}, u32[]{:S(2)}) collective-permute-start(f16[144,1024]{1,0:T(8,128)(2,1)S(1)} %convert_element_type.89), channel_id=1, source_target_pairs={{0,224},{32,0},{64,32},{96,64},{128,96},{160,128},{192,160},{224,1... | collective-permute-start | bytes 884744 | tf_op jit(solution)/shard_map/ppermute | solution.py:298
  65.7 16.8 %collective-permute-start.13 = (f16[144,1024]{1,0:T(8,128)(2,1)S(1)}, f16[144,1024]{1,0:T(8,128)(2,1)S(1)}, u32[]{:S(2)}, u32[]{:S(2)}) collective-permute-start(f16[144,1024]{1,0:T(8,128)(2,1)S(1)} %add_convert_fusion.2), channel_id=1, source_target_pairs={{0,32},{32,64},{64,96},{96,128},{128,160},{160,192},{192,224},{224... | collective-permute-start | bytes 884744 | tf_op jit(solution)/shard_map/ppermute | solution.py:298
  69.7 8.2 %collective-permute-start.3 = (f16[144,1024]{1,0:T(8,128)(2,1)S(1)}, f16[144,1024]{1,0:T(8,128)(2,1)S(1)}, u32[]{:S(2)}, u32[]{:S(2)}) collective-permute-start(f16[144,1024]{1,0:T(8,128)(2,1)S(1)} %add_convert_fusion.9), channel_id=1, source_target_pairs={{0,224},{32,0},{64,32},{96,64},{128,96},{160,128},{192,160},{224,1... | collective-permute-start | bytes 884744 | tf_op jit(solution)/shard_map/ppermute | solution.py:298
  73.1 8.6 %collective-permute-start.7 = (f16[144,1024]{1,0:T(8,128)(2,1)S(1)}, f16[144,1024]{1,0:T(8,128)(2,1)S(1)}, u32[]{:S(2)}, u32[]{:S(2)}) collective-permute-start(f16[144,1024]{1,0:T(8,128)(2,1)S(1)} %add_convert_fusion.6), channel_id=1, source_target_pairs={{0,32},{32,64},{64,96},{96,128},{128,160},{160,192},{192,224},{224... | collective-permute-start | bytes 884744 | tf_op jit(solution)/shard_map/ppermute | solution.py:298
  73.3 10.9 %collective-permute-start.10 = (f16[144,1024]{1,0:T(8,128)(2,1)S(1)}, f16[144,1024]{1,0:T(8,128)(2,1)S(1)}, u32[]{:S(2)}, u32[]{:S(2)}) collective-permute-start(f16[144,1024]{1,0:T(8,128)(2,1)S(1)} %add_convert_fusion.4), channel_id=1, source_target_pairs={{0,224},{32,0},{64,32},{96,64},{128,96},{160,128},{192,160},{224,1... | collective-permute-start | bytes 884744 | tf_op jit(solution)/shard_map/ppermute | solution.py:298
  78.0 12.6 %collective-permute-start.4 = (f16[144,1024]{1,0:T(8,128)(2,1)S(1)}, f16[144,1024]{1,0:T(8,128)(2,1)S(1)}, u32[]{:S(2)}, u32[]{:S(2)}) collective-permute-start(f16[144,1024]{1,0:T(8,128)(2,1)S(1)} %add_convert_fusion.8), channel_id=1, source_target_pairs={{0,224},{32,0},{64,32},{96,64},{128,96},{160,128},{192,160},{224,1... | collective-permute-start | bytes 884744 | tf_op jit(solution)/shard_map/ppermute | solution.py:298
  81.9 12.4 %collective-permute-start.8 = (f16[144,1024]{1,0:T(8,128)(2,1)S(1)}, f16[144,1024]{1,0:T(8,128)(2,1)S(1)}, u32[]{:S(2)}, u32[]{:S(2)}) collective-permute-start(f16[144,1024]{1,0:T(8,128)(2,1)S(1)} %add_convert_fusion.5), channel_id=1, source_target_pairs={{0,32},{32,64},{64,96},{96,128},{128,160},{160,192},{192,224},{224... | collective-permute-start | bytes 884744 | tf_op jit(solution)/shard_map/ppermute | solution.py:298
  82.6 11.5 %collective-permute-start.14 = (f16[144,1024]{1,0:T(8,128)(2,1)S(1)}, f16[144,1024]{1,0:T(8,128)(2,1)S(1)}, u32[]{:S(2)}, u32[]{:S(2)}) collective-permute-start(f16[144,1024]{1,0:T(8,128)(2,1)S(1)} %add_convert_fusion.1), channel_id=1, source_target_pairs={{0,32},{32,64},{64,96},{96,128},{128,160},{160,192},{192,224},{224... | collective-permute-start | bytes 884744 | tf_op jit(solution)/shard_map/ppermute | solution.py:298
  84.3 12.6 %collective-permute-start.11 = (f16[144,1024]{1,0:T(8,128)(2,1)S(1)}, f16[144,1024]{1,0:T(8,128)(2,1)S(1)}, u32[]{:S(2)}, u32[]{:S(2)}) collective-permute-start(f16[144,1024]{1,0:T(8,128)(2,1)S(1)} %add_convert_fusion.3), channel_id=1, source_target_pairs={{0,224},{32,0},{64,32},{96,64},{128,96},{160,128},{192,160},{224,1... | collective-permute-start | bytes 884744 | tf_op jit(solution)/shard_map/ppermute | solution.py:298
  90.6 12.6 %collective-permute-start.5 = (f16[144,1024]{1,0:T(8,128)(2,1)S(1)}, f16[144,1024]{1,0:T(8,128)(2,1)S(1)}, u32[]{:S(2)}, u32[]{:S(2)}) collective-permute-start(f16[144,1024]{1,0:T(8,128)(2,1)S(1)} %add_convert_fusion.7), channel_id=1, source_target_pairs={{0,224},{32,0},{64,32},{96,64},{128,96},{160,128},{192,160},{224,1... | collective-permute-start | bytes 884744 | tf_op jit(solution)/shard_map/ppermute | solution.py:298
  94.1 27.4 %copy-start = (bf16[1,1024,896]{2,1,0:T(8,128)(2,1)S(1)}, bf16[1,1024,896]{2,1,0:T(8,128)(2,1)}, u32[]{:S(2)}) copy-start(bf16[1,1024,896]{2,1,0:T(8,128)(2,1)} %refs_4_.3) | copy-start | bytes 5505028
  94.1 27.4 %copy-start.1 = (bf16[1024,896]{1,0:T(8,128)(2,1)S(1)}, bf16[1024,896]{1,0:T(8,128)(2,1)}, u32[]{:S(2)}) copy-start(bf16[1024,896]{1,0:T(8,128)(2,1)} %refs_5_.3) | copy-start | bytes 5505028
  94.2 9.0 %collective-permute-start.15 = (f16[144,1024]{1,0:T(8,128)(2,1)S(1)}, f16[144,1024]{1,0:T(8,128)(2,1)S(1)}, u32[]{:S(2)}, u32[]{:S(2)}) collective-permute-start(f16[144,1024]{1,0:T(8,128)(2,1)S(1)} %add_convert_fusion), channel_id=1, source_target_pairs={{0,32},{32,64},{64,96},{96,128},{128,160},{160,192},{192,224},{224... | collective-permute-start | bytes 884744 | tf_op jit(solution)/shard_map/ppermute | solution.py:298
  103.5 7.6 %collective-permute-start.18 = (bf16[144,1024]{1,0:T(8,128)(2,1)S(1)}, bf16[144,1024]{1,0:T(8,128)(2,1)S(1)}, u32[]{:S(2)}, u32[]{:S(2)}) collective-permute-start(bf16[144,1024]{1,0:T(8,128)(2,1)S(1)} %multiply_convert_fusion.refs_1_), channel_id=1, source_target_pairs={{0,32},{32,64},{64,96},{96,128},{128,160},{160,192},{192,224},{224... | collective-permute-start | bytes 884744 | tf_op jit(solution)/shard_map/ppermute | solution.py:334
  103.6 7.5 %collective-permute-start.16 = (bf16[144,1024]{1,0:T(8,128)(2,1)S(1)}, bf16[144,1024]{1,0:T(8,128)(2,1)S(1)}, u32[]{:S(2)}, u32[]{:S(2)}) collective-permute-start(bf16[144,1024]{1,0:T(8,128)(2,1)S(1)} %multiply_convert_fusion.refs_1_), channel_id=1, source_target_pairs={{0,224},{32,0},{64,32},{96,64},{128,96},{160,128},{192,160},{224,1... | collective-permute-start | bytes 884744 | tf_op jit(solution)/shard_map/ppermute | solution.py:333
  111.1 7.4 %collective-permute-start.19 = (bf16[144,1024]{1,0:T(8,128)(2,1)S(1)}, bf16[144,1024]{1,0:T(8,128)(2,1)S(1)}, u32[]{:S(2)}, u32[]{:S(2)}) collective-permute-start(bf16[144,1024]{1,0:T(8,128)(2,1)S(1)} %collective-permute-done.18.refs_2_), channel_id=1, source_target_pairs={{0,32},{32,64},{64,96},{96,128},{128,160},{160,192},{192,224},{224... | collective-permute-start | bytes 884744 | tf_op jit(solution)/shard_map/ppermute | solution.py:334
  111.1 7.4 %collective-permute-start.17 = (bf16[144,1024]{1,0:T(8,128)(2,1)S(1)}, bf16[144,1024]{1,0:T(8,128)(2,1)S(1)}, u32[]{:S(2)}, u32[]{:S(2)}) collective-permute-start(bf16[144,1024]{1,0:T(8,128)(2,1)S(1)} %collective-permute-done.16.refs_0_), channel_id=1, source_target_pairs={{0,224},{32,0},{64,32},{96,64},{128,96},{160,128},{192,160},{224,1... | collective-permute-start | bytes 884744 | tf_op jit(solution)/shard_map/ppermute | solution.py:333
  118.5 13.1 %collective-permute-start.24 = (bf16[144,1024]{1,0:T(8,128)(2,1)S(1)}, bf16[144,1024]{1,0:T(8,128)(2,1)S(1)}, u32[]{:S(2)}, u32[]{:S(2)}) collective-permute-start(bf16[144,1024]{1,0:T(8,128)(2,1)S(1)} %collective-permute-done.19.refs_3_), channel_id=1, source_target_pairs={{0,32},{32,64},{64,96},{96,128},{128,160},{160,192},{192,224},{224... | collective-permute-start | bytes 884744 | tf_op jit(solution)/shard_map/ppermute | solution.py:334
  118.5 13.2 %collective-permute-start.23 = (bf16[144,1024]{1,0:T(8,128)(2,1)S(1)}, bf16[144,1024]{1,0:T(8,128)(2,1)S(1)}, u32[]{:S(2)}, u32[]{:S(2)}) collective-permute-start(bf16[144,1024]{1,0:T(8,128)(2,1)S(1)} %collective-permute-done.17.refs_1_), channel_id=1, source_target_pairs={{0,224},{32,0},{64,32},{96,64},{128,96},{160,128},{192,160},{224,1... | collective-permute-start | bytes 884744 | tf_op jit(solution)/shard_map/ppermute | solution.py:333
  123.1 20.3 %collective-permute-start.20 = (f32[2,144,896]{2,1,0:T(8,128)S(1)}, f32[2,144,896]{2,1,0:T(8,128)}, u32[]{:S(2)}, u32[]{:S(2)}) collective-permute-start(f32[2,144,896]{2,1,0:T(8,128)S(1)} %get-tuple-element.48), channel_id=1, source_target_pairs={{0,1},{1,0},{2,3},{3,2},{4,5},{5,4},{6,7},{7,6},{8,9},{9,8},{10,11... | collective-permute-start | bytes 3096584 | tf_op jit(solution)/shard_map/ppermute | solution.py:343
  131.7 5.3 %collective-permute-start.26 = (bf16[72,1024]{1,0:T(8,128)(2,1)S(1)}, bf16[72,1024]{1,0:T(8,128)(2,1)S(1)}, u32[]{:S(2)}, u32[]{:S(2)}) collective-permute-start(bf16[72,1024]{1,0:T(8,128)(2,1)S(1)} %slice.47), channel_id=1, source_target_pairs={{0,32},{32,64},{64,96},{96,128},{128,160},{160,192},{192,224},{224... | collective-permute-start | bytes 442376 | tf_op jit(solution)/shard_map/ppermute | solution.py:338
  131.8 5.2 %collective-permute-start.25 = (bf16[72,1024]{1,0:T(8,128)(2,1)S(1)}, bf16[72,1024]{1,0:T(8,128)(2,1)S(1)}, u32[]{:S(2)}, u32[]{:S(2)}) collective-permute-start(bf16[72,1024]{1,0:T(8,128)(2,1)S(1)} %slice.46), channel_id=1, source_target_pairs={{0,224},{32,0},{64,32},{96,64},{128,96},{160,128},{192,160},{224,1... | collective-permute-start | bytes 442376 | tf_op jit(solution)/shard_map/ppermute | solution.py:337
  139.6 10.7 %collective-permute-start.27 = (f32[2,144,896]{2,1,0:T(8,128)}, f32[2,144,896]{2,1,0:T(8,128)}, u32[]{:S(2)}, u32[]{:S(2)}) collective-permute-start(f32[2,144,896]{2,1,0:T(8,128)} %get-tuple-element.50), channel_id=1, source_target_pairs={{0,1},{1,0},{2,3},{3,2},{4,5},{5,4},{6,7},{7,6},{8,9},{9,8},{10,11... | collective-permute-start | bytes 3096584 | tf_op jit(solution)/shard_map/ppermute | solution.py:343
  143.5 6.8 %copy-start.11 = (s32[2]{0:T(128)S(1)}, s32[2]{0:T(128)}, u32[]{:S(2)}) copy-start(s32[2]{0:T(128)} %constant.45.clone) | copy-start | bytes 28
  143.5 6.8 %copy-start.12 = (s32[2]{0:T(128)S(1)}, s32[2]{0:T(128)}, u32[]{:S(2)}) copy-start(s32[2]{0:T(128)} %constant.44.clone) | copy-start | bytes 28
  144.8 1.0 copy-start.8
  146.7 14.2 %all-to-all-start.2 = ((bf16[16,16,896]{2,1,0:T(8,128)(2,1)}), bf16[16,16,896]{2,1,0:T(8,128)(2,1)S(1)}, u32[]{:S(2)}, u32[]{:S(2)}) async-start(bf16[16,16,896]{2,1,0:T(8,128)(2,1)} %copy_bitcast_fusion.3), calls=%async_computation.2 | async-start | bytes 917504 | tf_op jit(solution)/shard_map/all_to_all | solution.py:346
  150.3 14.1 %copy-start.9 = (s32[2]{0:T(128)S(1)}, s32[2]{0:T(128)}, u32[]{:S(2)}) copy-start(s32[2]{0:T(128)} %constant.47.clone) | copy-start | bytes 28
  150.3 14.1 %copy-start.10 = (s32[2]{0:T(128)S(1)}, s32[2]{0:T(128)}, u32[]{:S(2)}) copy-start(s32[2]{0:T(128)} %constant.46.clone) | copy-start | bytes 28
  160.8 13.3 %all-to-all-start.3 = ((bf16[16,16,896]{2,1,0:T(8,128)(2,1)}), bf16[16,16,896]{2,1,0:T(8,128)(2,1)S(1)}, u32[]{:S(2)}, u32[]{:S(2)}) async-start(bf16[16,16,896]{2,1,0:T(8,128)(2,1)} %copy_bitcast_fusion.2), calls=%async_computation.3 | async-start | bytes 917504 | tf_op jit(solution)/shard_map/all_to_all | solution.py:346
  166.6 13.3 %collective-permute-start.22 = (bf16[16,896]{1,0:T(8,128)(2,1)S(1)}, bf16[16,896]{1,0:T(8,128)(2,1)S(1)}, u32[]{:S(2)}, u32[]{:S(2)}) collective-permute-start(bf16[16,896]{1,0:T(8,128)(2,1)S(1)} %get-tuple-element.53), channel_id=1, source_target_pairs={{0,64},{1,193},{32,96},{33,225},{64,128},{65,1},{96,160},{97,33},{... | collective-permute-start | bytes 86024 | tf_op jit(solution)/shard_map/ppermute | solution.py:351
  168.3 12.0 %collective-permute-start.21 = (bf16[16,896]{1,0:T(8,128)(2,1)S(1)}, bf16[16,896]{1,0:T(8,128)(2,1)S(1)}, u32[]{:S(2)}, u32[]{:S(2)}) collective-permute-start(bf16[16,896]{1,0:T(8,128)(2,1)S(1)} %get-tuple-element.54), channel_id=1, source_target_pairs={{0,32},{1,225},{32,64},{33,1},{64,96},{65,33},{96,128},{97,65},{12... | collective-permute-start | bytes 86024 | tf_op jit(solution)/shard_map/ppermute | solution.py:351
  175.3 8.8 %collective-permute-start.29 = (bf16[16,896]{1,0:T(8,128)(2,1)S(1)}, bf16[16,896]{1,0:T(8,128)(2,1)S(1)}, u32[]{:S(2)}, u32[]{:S(2)}) collective-permute-start(bf16[16,896]{1,0:T(8,128)(2,1)S(1)} %get-tuple-element.51), channel_id=1, source_target_pairs={{0,0},{1,129},{32,32},{33,161},{64,64},{65,193},{96,96},{97,225},{... | collective-permute-start | bytes 86024 | tf_op jit(solution)/shard_map/ppermute | solution.py:351
  178.1 7.1 %collective-permute-start.28 = (bf16[16,896]{1,0:T(8,128)(2,1)S(1)}, bf16[16,896]{1,0:T(8,128)(2,1)S(1)}, u32[]{:S(2)}, u32[]{:S(2)}) collective-permute-start(bf16[16,896]{1,0:T(8,128)(2,1)S(1)} %get-tuple-element.52), channel_id=1, source_target_pairs={{0,96},{1,161},{32,128},{33,193},{64,160},{65,225},{96,192},{97,1}... | collective-permute-start | bytes 86024 | tf_op jit(solution)/shard_map/ppermute | solution.py:351
  179.9 5.4 %collective-permute-start.31 = (bf16[16,896]{1,0:T(8,128)(2,1)S(1)}, bf16[16,896]{1,0:T(8,128)(2,1)S(1)}, u32[]{:S(2)}, u32[]{:S(2)}) collective-permute-start(bf16[16,896]{1,0:T(8,128)(2,1)S(1)} %collective-permute-done.22.refs_1_), channel_id=1, source_target_pairs={{0,1},{1,0},{2,3},{3,2},{4,5},{5,4},{6,7},{7,6},{8,9},{9,8},{10,11... | collective-permute-start | bytes 86024 | tf_op jit(solution)/shard_map/ppermute | solution.py:355
  180.3 5.0 %collective-permute-start.30 = (bf16[16,896]{1,0:T(8,128)(2,1)S(1)}, bf16[16,896]{1,0:T(8,128)(2,1)S(1)}, u32[]{:S(2)}, u32[]{:S(2)}) collective-permute-start(bf16[16,896]{1,0:T(8,128)(2,1)S(1)} %collective-permute-done.21.refs_0_), channel_id=1, source_target_pairs={{0,1},{1,0},{2,3},{3,2},{4,5},{5,4},{6,7},{7,6},{8,9},{9,8},{10,11... | collective-permute-start | bytes 86024 | tf_op jit(solution)/shard_map/ppermute | solution.py:355
  184.2 1.2 collective-permute-start.33
  185.2 1.2 collective-permute-start.32

commit v2 on v1

--- a/solution.py
+++ b/solution.py
@@ -19,12 +19,14 @@
 ROWS = EXPERTS * CAP
 CHUNK = ROWS + PADT
 FFH = 1024
+EARLY = 3
+CUT = FFH // 2
 NT = 256
 ORDER = (3, 4, 5, 6, 7, 0, 1, 2)
 SCALE = 16.0
 LINK = jnp.float16
 
-PARAMS = pltpu.CompilerParams(vmem_limit_bytes=24 * 1024 * 1024)
+PARAMS = pltpu.CompilerParams(vmem_limit_bytes=16 * 1024 * 1024)
 VMEM = pl.BlockSpec(memory_space=pltpu.VMEM)
 SMEM = pl.BlockSpec(memory_space=pltpu.SMEM)
 SWAP = [(0, 1), (1, 0)]
@@ -46,8 +48,14 @@
     return jnp.dot(a, b, preferred_element_type=jnp.float32)
 
 
-def prep_kernel(c_ref, x_ref, ids_ref, w_ref, out_ref):
+def prep_kernel(c_ref, x_hbm, ids_hbm, w_hbm, out_ref, x_ref, ids_ref, w_ref, sems):
     first = c_ref[0] == 0
+    pairs = ((ids_hbm, ids_ref), (w_hbm, w_ref), (x_hbm, x_ref))
+    copies = [pltpu.make_async_copy(a, b, sems.at[i]) for i, (a, b) in enumerate(pairs)]
+    for copy in copies:
+        copy.start()
+    for copy in copies:
+        copy.wait()
     w = w_ref[...]
     hi = w.astype(jnp.bfloat16)
     rest = w - hi.astype(jnp.float32)
@@ -58,7 +66,8 @@
     start = jnp.where(first, 64, 0)
     ext = jnp.zeros((TOK, 128), jnp.float32)
     for i, v in enumerate((ids_ref[...].astype(jnp.float32).astype(jnp.bfloat16), hi, mid, low)):
-        ext = ext + fdot(v, (lane == start + TOP * i + part).astype(jnp.bfloat16))
+        spread = (lane == start + TOP * i + part).astype(jnp.bfloat16)
+        ext = ext + lax.dot_general(v, spread, (((0,), (0,)), ((), ())), preferred_element_type=jnp.float32)
     lanes = lax.broadcasted_iota(jnp.int32, (TOK, 128), 1)
     routing = lanes // 64 == jnp.where(first, 1, 0)
     for b in range(ZN):
@@ -81,8 +90,14 @@
     return pl.pallas_call(
         prep_kernel,
         out_shape=jax.ShapeDtypeStruct((ZN, TOK, WIDE), jnp.bfloat16),
-        in_specs=[SMEM, VMEM, VMEM, VMEM],
+        in_specs=[SMEM] + [pl.BlockSpec(memory_space=pltpu.HBM)] * 3,
         out_specs=VMEM,
+        scratch_shapes=[
+            pltpu.VMEM((TOK, ZN * BLOCK), jnp.bfloat16),
+            pltpu.VMEM((TOP, TOK), jnp.int32),
+            pltpu.VMEM((TOP, TOK), jnp.float32),
+            pltpu.SemaphoreType.DMA((3,)),
+        ],
         compiler_params=PARAMS,
         name="prep",
     )(c, x, ids, w)
@@ -176,9 +191,12 @@
 
 def down_kernel(c_ref, *refs):
     xs, (wd_ref, sd_ref, keep_ref, send_ref) = refs[:-4], refs[-4:]
-    n = len(xs) // 2
-    full = fdot(jnp.concatenate([x[:ROWS] for x in xs], axis=0), wd_ref[0])
-    shared = fdot(jnp.concatenate([x[ROWS:] for x in xs], axis=0), sd_ref[...])
+    sides = (xs[::2], xs[1::2])
+    n = len(xs) // 4
+    full, shared = 0.0, 0.0
+    for side, cols in zip(sides, (slice(0, CUT), slice(CUT, FFH))):
+        full = full + fdot(jnp.concatenate([x[:ROWS] for x in side], axis=0), wd_ref[0, cols])
+        shared = shared + fdot(jnp.concatenate([x[ROWS:] for x in side], axis=0), sd_ref[cols])
 
     def store(ref, i, at):
         ref[i, :ROWS] = full[at * ROWS : (at + 1) * ROWS]
@@ -198,7 +216,7 @@
 
 
 def down_dots(c, xs, wd, sd):
-    n = len(xs) // 2
+    n = len(xs) // 4
     return pl.pallas_call(
         down_kernel,
         out_shape=(
@@ -215,20 +233,48 @@
     )(c, *xs, wd, sd)
 
 
-def combine_kernel(zs_ref, ext_ref, back_ref, shared_ref, out_ref):
+def settle_kernel(keep_ref, came_ref, *refs):
+    before, (rows_ref, shared_ref) = refs[:-2], refs[-2:]
+    at = 0
+    if before:
+        at = 2 * CAP
+        rows_ref[:, :at, :] = before[0][...]
+    for i in range(2):
+        total = keep_ref[i, :ROWS] + came_ref[i, :ROWS]
+        rows_ref[:, at + i * CAP : at + (i + 1) * CAP, :] = total.reshape(EXPERTS, CAP, BLOCK).astype(jnp.bfloat16)
+        shared_ref[i * PADT : (i + 1) * PADT] = keep_ref[i, ROWS:] + came_ref[i, ROWS:]
+
+
+def settle(keep, came, *before):
+    return pl.pallas_call(
+        settle_kernel,
+        out_shape=(
+            jax.ShapeDtypeStruct((EXPERTS, (2 + 2 * len(before)) * CAP, BLOCK), jnp.bfloat16),
+            jax.ShapeDtypeStruct((2 * PADT, BLOCK), jnp.float32),
+        ),
+        in_specs=[VMEM] * (2 + len(before)),
+        out_specs=(VMEM, VMEM),
+        compiler_params=PARAMS,
+        name="settle",
+    )(keep, came, *before)
+
+
+def combine_kernel(zs_ref, ext_ref, back_ref, near_ref, far_ref, out_ref):
     n = ZN * TOK
-    rows = 2 * PADT
-    cols = 2 * ROWS
+    rows = 4 * PADT
+    cols = 4 * ROWS
     t = lax.broadcasted_iota(jnp.int32, (rows, n), 0)
     r = lax.broadcasted_iota(jnp.int32, (rows, n), 1)
-    zs = jnp.where(t < PADT, zs_ref[0], zs_ref[1])
+    zs = jnp.full((rows, n), zs_ref[3], jnp.int32)
+    for i in range(3):
+        zs = jnp.where(t // PADT == i, zs_ref[i], zs)
     pick = ((r == zs * TOK + t % PADT) & (t % PADT < TOK)).astype(jnp.bfloat16)
     ext = fdot(pick, ext_ref[...])
     weight = (ext[:, 72:80] + ext[:, 80:88]) + ext[:, 88:96]
     column = lax.broadcasted_iota(jnp.int32, (rows, cols), 1)
     row = lax.broadcasted_iota(jnp.int32, (rows, cols), 0)
-    live = (row % PADT < TOK) & (row // PADT == (column // CAP) % 2)
-    owner = (column // (2 * CAP)).astype(jnp.float32)
+    live = (row % PADT < TOK) & (row // PADT == (column // CAP) % 4)
+    owner = (column // (4 * CAP)).astype(jnp.float32)
     slot = (column % CAP).astype(jnp.float32)
     member = jnp.zeros((rows, cols), jnp.float32)
     scale = jnp.zeros((rows, cols), jnp.float32)
@@ -247,29 +293,32 @@
     low = (rest - mid.astype(jnp.float32)).astype(jnp.bfloat16)
     back = back_ref[...]
     total = (fdot(low, back) + fdot(mid, back)) + fdot(hi, back)
-    out_ref[...] = (shared_ref[...] + total).astype(jnp.bfloat16)
-
-
-def combine(zs, ext, back, shared):
+    out_ref[: 2 * PADT] = (near_ref[...] + total[: 2 * PADT]).astype(jnp.bfloat16)
+    out_ref[2 * PADT :] = (far_ref[...] + total[2 * PADT :]).astype(jnp.bfloat16)
+
+
+def combine(zs, ext, back, near, far):
     return pl.pallas_call(
         combine_kernel,
-        out_shape=jax.ShapeDtypeStruct((2 * PADT, BLOCK), jnp.bfloat16),
-        in_specs=[SMEM, VMEM, VMEM, VMEM],
+        out_shape=jax.ShapeDtypeStruct((4 * PADT, BLOCK), jnp.bfloat16),
+        in_specs=[SMEM, VMEM, VMEM, VMEM, VMEM],
         out_specs=VMEM,
         compiler_params=PARAMS,
         name="combine",
-    )(zs, ext, back, shared)
+    )(zs, ext, back, near, far)
 
 
 def assemble_kernel(s_ref, *refs):
     out_ref = refs[-1]
     z = s_ref[0]
-    a1, a2, b3, b0, o1, o2, o3, o0 = refs[:-1]
+    held_ref, came_ref = refs[:-1]
+    a1, a2, b3, b0 = [held_ref[i * PADT : i * PADT + TOK] for i in range(4)]
+    o1, o2, o3, o0 = [came_ref[i * PADT : i * PADT + TOK] for i in range(4)]
 
     def put(parts):
-        for i, ref in enumerate(parts):
+        for i, part in enumerate(parts):
             at = pl.multiple_of(((z + i) % ZN) * BLOCK, 128)
-            out_ref[:, pl.ds(at, BLOCK)] = ref[:TOK]
+            out_ref[:, pl.ds(at, BLOCK)] = part
 
     @pl.when(s_ref[1] == 0)
     def _():
@@ -303,23 +352,20 @@
     z = lax.axis_index("dp")
     c = lax.axis_index("tensor")
     c1, zc = c.reshape(1), jnp.stack([z, c])
-    pieces = prep(c1, tokens, ids, weights)
+    pieces = prep(c1, tokens, ids.T, weights.T)
     column = lax.all_to_all(pieces, "dp", 0, 0, tiled=True).reshape(ZN * TOK, WIDE)
     packed, shared_own, ext = pack(zc, column)
     shared_oth = lax.ppermute(shared_own, "tensor", SWAP)
     arrived = lax.all_to_all(packed, "expert", 0, 0, tiled=True)
     other = lax.ppermute(arrived, "tensor", SWAP)
-
-    def by_chunk(a):
-        a = a.reshape(EXPERTS, ZN, CAP, HALF)
-        return jnp.moveaxis(a, 1, 0).reshape(ZN, ROWS, HALF)
-
-    own, oth = by_chunk(arrived), by_chunk(other)
+    own, oth = [
+        jnp.moveaxis(a.reshape(EXPERTS, ZN, CAP, HALF), 1, 0).reshape(ZN, ROWS, HALF) for a in (arrived, other)
+    ]
     args = (c1, own, oth, shared_own, shared_oth, wg, wu, sg, su)
-    early = up_dots(0, 3, *args)
-    late = up_dots(3, 5, *args)
-    gate = dict(zip(ORDER, early[:3] + late[:5]))
-    up = dict(zip(ORDER, early[3:] + late[5:]))
+    early = up_dots(0, EARLY, *args)
+    late = up_dots(EARLY, ZN - EARLY, *args)
+    gate = dict(zip(ORDER, early[:EARLY] + late[: ZN - EARLY]))
+    up = dict(zip(ORDER, early[EARLY:] + late[ZN - EARLY :]))
     g_down = ring([gate[k] for k in (4, 3, 2, 1)], -1)
     u_up = ring([up[k] for k in (4, 5, 6, 7)], 1)
     u_down = ring([up[k] for k in (3, 2, 1)], -1)
@@ -327,33 +373,33 @@
     g = (gate[0] + (g_down + g_up)) * (1.0 / SCALE)
     u = (up[0] + (u_down + u_up)) * (1.0 / SCALE)
     hidden = (jax.nn.silu(g) * u).astype(jnp.bfloat16)
-    got = {0: hidden}
-    down, above = hidden, hidden
-    for j in range(1, 4):
-        down = lax.ppermute(down, "dp", shifted(-1))
-        above = lax.ppermute(above, "dp", shifted(1))
-        got[ZN - j], got[j] = down, above
-    cut = CHUNK // 2
-    down = lax.ppermute(down[:cut], "dp", shifted(-1))
-    above = lax.ppermute(above[cut:], "dp", shifted(1))
-    got[4] = jnp.concatenate([down, above])
-    held = {}
-    for a, b, sends in (((7, 6), (1, 2), ((1, 1), (2, 2))), ((5, 0), (3, 4), ((3, 3), (0, 4)))):
-        keep, send = down_dots(c1, [got[k] for k in a + b], wd, sd)
-        total = keep + lax.ppermute(send, "tensor", SWAP)
-        rows = total[:, :ROWS].astype(jnp.bfloat16).reshape(2, EXPERTS, CAP, BLOCK)
-        rows = jnp.moveaxis(rows, 0, 1).reshape(EXPERTS, 2 * CAP, BLOCK)
-        back = lax.all_to_all(rows, "expert", 0, 0, tiled=True).reshape(2 * ROWS, BLOCK)
-        ks = jnp.where(c == 0, jnp.array(a), jnp.array(b))
-        shared = total[:, ROWS:].reshape(2 * PADT, BLOCK)
-        mixed = combine((z - ks) % ZN, ext, back, shared)
-        for i, (to, fro) in enumerate(sends):
-            held[to] = lax.ppermute(mixed[i * PADT : (i + 1) * PADT], ("dp", "tensor"), paired(to, fro))
-    parts = [held[1], held[2], held[3], held[0]]
-    others = []
-    for p in parts:
-        others.append(lax.ppermute(p, "tensor", SWAP))
-    return assemble(zc, *parts, *others)
+    top, tail = hidden[:, :CUT], hidden[:, CUT:]
+    got = {0: (top, tail)}
+    pd, pu, qd, qu = top, top, tail, tail
+    for j in range(1, 5):
+        pd = lax.ppermute(pd, "dp", shifted(-1))
+        qu = lax.ppermute(qu, "dp", shifted(1))
+        if j < 4:
+            qd = lax.ppermute(qd, "dp", shifted(-1))
+            pu = lax.ppermute(pu, "dp", shifted(1))
+            got[ZN - j], got[j] = (pd, qd), (pu, qu)
+        else:
+            got[4] = (pd, qu)
+    rows, shares = (), []
+    for a, b in (((7, 6), (1, 2)), ((5, 0), (3, 4))):
+        keep, send = down_dots(c1, [p for k in a + b for p in got[k]], wd, sd)
+        came = lax.ppermute(send, "tensor", SWAP)
+        *rows, shared = settle(keep, came, *rows)
+        shares.append(shared)
+    back = lax.all_to_all(rows[0], "expert", 0, 0, tiled=True).reshape(4 * ROWS, BLOCK)
+    ks = jnp.where(c == 0, jnp.array((7, 6, 5, 0)), jnp.array((1, 2, 3, 4)))
+    mixed = combine((z - ks) % ZN, ext, back, *shares)
+    held = []
+    for i, (to, fro) in enumerate(((1, 1), (2, 2), (3, 3), (0, 4))):
+        held.append(lax.ppermute(mixed[i * PADT : (i + 1) * PADT], ("dp", "tensor"), paired(to, fro)))
+    held = jnp.concatenate(held)
+    others = lax.ppermute(held, "tensor", SWAP)
+    return assemble(zc, held, others)
 
 
 def solution(mesh):
@@ -368,6 +414,4 @@
         P("dp", "tensor"),
         P("tensor", "dp"),
     )
-    return jax.shard_map(
-        layer, mesh=mesh, in_specs=placed, out_specs=P(("dp", "expert"), None), check_vma=False
-    )
+    return jax.shard_map(layer, mesh=mesh, in_specs=placed, out_specs=P(("dp", "expert"), None), check_vma=False)

time: 188 us -> 179 us (0.952)
  local copies, waits for them, and re-layouts: 7.86 us -> 4.11 us
  other arithmetic: 4.16 us -> 1.44 us
  waiting for transfers between devices: 58 us -> 55.5 us
    ppermute x4, waiting for transfers between devices: 4.83 us -> 1.11 us  [layer(): lax.ppermute(mixed[i * PADT:(i + 1) * PADT], ('dp', 'tensor'), paired(to,...]
    all_to_all x2 -> x1, starting transfers between devices: 7.12 us -> 3.63 us  [layer(): lax.all_to_all(rows[0], 'expert', 0, 0, tiled=True).reshape(4 * ROWS, BLOCK)]
    all_to_all x2 -> x1, waiting for transfers between devices: 12.3 us -> 15.1 us  [layer(): lax.all_to_all(rows[0], 'expert', 0, 0, tiled=True).reshape(4 * ROWS, BLOCK)]
    add x2 -> x0, other arithmetic: 2.68 us -> none  [layer(): total = keep + lax.ppermute(send, 'tensor', SWAP)]
    ppermute x4, starting transfers between devices: 8.1 us -> 10.4 us  [layer(): lax.ppermute(mixed[i * PADT:(i + 1) * PADT], ('dp', 'tensor'), paired(to,...]
    ppermute x14 -> x17, waiting for transfers between devices: 12.1 us -> 10.5 us  [the longest x4 5.18 us: layer(): qu = lax.ppermute(qu, 'dp', shifted(1))]
    ppermute x14 -> x17, starting transfers between devices: 25.2 us -> 26.4 us  [the longest x4 12.3 us: layer(): pd = lax.ppermute(pd, 'dp', shifted(-1))]
    unnamed x28 -> x27, local copies, waits for them, and re-layouts: 5.03 us -> 3.86 us
  transfers between devices with their start and end apart: 37 -> 39, of which waited for: 19 -> 21; matrix products, arithmetic and copies ran while one was open for 3% -> 1% of each run, Pallas kernels for 6% -> 5%
where the time goes in v2:
time: 179 us
  starting transfers between devices  76.1 us (43%)
  waiting for transfers between devices  55.5 us (31%)
  blocking collectives  21.6 us (12%)
  Pallas kernels  19.4 us (11%)
  local copies, waits for them, and re-layouts  4.11 us (2%)
    ppermute x14, starting transfers between devices, ring(): total = lax.ppermute(total.astype(LINK), 'dp', shifted(shift))  23.2 us
    all_to_all x1, blocking collectives, layer(): arrived = lax.all_to_all(packed, 'expert', 0, 0, tiled=True)  21.6 us
    ppermute x14, waiting for transfers between devices, ring(): total = lax.ppermute(total.astype(LINK), 'dp', shifted(shift))  18.9 us
    all_to_all x1, waiting for transfers between devices, layer(): lax.all_to_all(rows[0], 'expert', 0, 0, tiled=True).reshape(4 * ROWS, BLOCK)  15.1 us
    ppermute x4, starting transfers between devices, layer(): pd = lax.ppermute(pd, 'dp', shifted(-1))  12.3 us
    ppermute x4, starting transfers between devices, layer(): lax.ppermute(mixed[i * PADT:(i + 1) * PADT], ('dp', 'tensor'), paired(to,...  10.4 us
    ppermute x2, starting transfers between devices, layer(): came = lax.ppermute(send, 'tensor', SWAP)  9.62 us
    pallas_call x2, Pallas kernels, up_dots(): pl.pallas_call(functools.partial(up_kernel, first, count), grid=(FFH // N...  9.55 us
  transfers between devices with their start and end apart: 39, of which 21 were waited for; matrix products, arithmetic and copies ran while one was open for 1% of the time, Pallas kernels for 5%

profile of v2, /device:TPU:1, one launch (start us, length us, event | category | flops | bytes accessed | tf_op | source)
XLA Modules:
  0.0 178.5 jit_solution(9476263385376295412)
XLA Ops:
  0.0 0.9 copy-done.7
  0.9 0.7 copy-done.8
  1.6 0.7 copy-done.9
  2.3 1.2 prep.1
  3.5 9.0 %all-to-all-start = ((bf16[8,12,512]{2,1,0:T(8,128)(2,1)}), bf16[8,12,512]{2,1,0:T(8,128)(2,1)S(1)}, u32[]{:S(2)}, u32[]{:S(2)}) async-start(bf16[8,12,512]{2,1,0:T(8,128)(2,1)} %prep.1), calls=%async_computation | async-start | bytes 262144 | tf_op jit(solution)/shard_map/all_to_all | solution.py:356
  12.6 7.7 %all-to-all-done = bf16[8,12,512]{2,1,0:T(8,128)(2,1)S(1)} async-done(((bf16[8,12,512]{2,1,0:T(8,128)(2,1)}), bf16[8,12,512]{2,1,0:T(8,128)(2,1)S(1)}, u32[]{:S(2)}, u32[]{:S(2)}) %all-to-all-start) | async-done | bytes 98336 | tf_op jit(solution)/shard_map/all_to_all | solution.py:356
  20.3 1.3 pack.1
  21.6 21.6 %all_to_all.15 = bf16[16,64,448]{2,1,0:T(8,128)(2,1)S(1)} all-to-all(bf16[16,64,448]{2,1,0:T(8,128)(2,1)S(1)} %get-tuple-element.33), channel_id=1, replica_groups=mesh['dp'=8,'expert'=16,'tensor'=2] {'expert'}, dimensions={0} | all-to-all | bytes 1835008 | tf_op jit(solution)/shard_map/all_to_all | solution.py:359
  43.2 3.3 %collective-permute-start = (bf16[16,64,448]{2,1,0:T(8,128)(2,1)S(1)}, bf16[16,64,448]{2,1,0:T(8,128)(2,1)S(1)}, u32[]{:S(2)}, u32[]{:S(2)}) collective-permute-start(bf16[16,64,448]{2,1,0:T(8,128)(2,1)S(1)} %all_to_all.15), channel_id=1, source_target_pairs={{0,1},{1,0},{2,3},{3,2},{4,5},{5,4},{6,7},{7,6},{8,9},{9,8},{10,11... | collective-permute-start | bytes 2752520 | tf_op jit(solution)/shard_map/ppermute | solution.py:360
  46.6 0.1 copy_bitcast_fusion.1.own_ref
  46.7 2.1 %collective-permute-done = bf16[16,64,448]{2,1,0:T(8,128)(2,1)S(1)} collective-permute-done((bf16[16,64,448]{2,1,0:T(8,128)(2,1)S(1)}, bf16[16,64,448]{2,1,0:T(8,128)(2,1)S(1)}, u32[]{:S(2)}, u32[]{:S(2)}) %collective-permute-start) | collective-permute-done | bytes 917536 | tf_op jit(solution)/shard_map/ppermute | solution.py:360
  48.8 0.1 copy_bitcast_fusion.oth_ref
  49.0 1.5 copy-done.5
  50.5 4.1 %shard_map.110 = (f32[144,1024]{1,0:T(8,128)S(1)}, f32[144,1024]{1,0:T(8,128)S(1)}, f32[144,1024]{1,0:T(8,128)S(1)}, f32[144,1024]{1,0:T(8,128)S(1)}, f32[144,1024]{1,0:T(8,128)S(1)}, /*index=5*/f32[144,1024]{1,0:T(8,128)S(1)}) custom-call(s32[1]{0:T(128)} %bitcast.1.c_ref, bf16[8,128,448]{2,1,0:T(8,128)(2,1)S(1)} %copy_bitcast_fusion.1.own_ref, ...), custom_call_target="tpu_custom_call" | custom-call | flops 1585446912 | bytes 7340032 | tf_op jit(solution)/shard_map/pallas_call | solution.py:169
  54.7 0.7 collective-permute-start.12
  55.5 2.1 %collective-permute-start.9 = (f16[144,1024]{1,0:T(8,128)(2,1)S(1)}, f16[144,1024]{1,0:T(8,128)(2,1)S(1)}, u32[]{:S(2)}, u32[]{:S(2)}) collective-permute-start(f16[144,1024]{1,0:T(8,128)(2,1)S(1)} %convert_element_type.101), channel_id=1, source_target_pairs={{0,224},{32,0},{64,32},{96,64},{128,96},{160,128},{192,160},{224,1... | collective-permute-start | bytes 884744 | tf_op jit(solution)/shard_map/ppermute | solution.py:347
  57.7 2.7 %collective-permute-start.2 = (f16[144,1024]{1,0:T(8,128)(2,1)S(1)}, f16[144,1024]{1,0:T(8,128)(2,1)S(1)}, u32[]{:S(2)}, u32[]{:S(2)}) collective-permute-start(f16[144,1024]{1,0:T(8,128)(2,1)S(1)} %convert_element_type.87), channel_id=1, source_target_pairs={{0,224},{32,0},{64,32},{96,64},{128,96},{160,128},{192,160},{224,1... | collective-permute-start | bytes 884744 | tf_op jit(solution)/shard_map/ppermute | solution.py:347
  60.3 5.4 %shard_map.109 = (f32[144,1024]{1,0:T(8,128)S(1)}, f32[144,1024]{1,0:T(8,128)S(1)}, f32[144,1024]{1,0:T(8,128)S(1)}, f32[144,1024]{1,0:T(8,128)S(1)}, f32[144,10...) custom-call(s32[1]{0:T(128)} %bitcast.1.c_ref, ...), custom_call_target="tpu_custom_call" | custom-call | flops 2642411520 | bytes 7340032 | tf_op jit(solution)/shard_map/pallas_call | solution.py:169
  66.0 3.9 %collective-permute-done.2 = f16[144,1024]{1,0:T(8,128)(2,1)S(1)} collective-permute-done((f16[144,1024]{1,0:T(8,128)(2,1)S(1)}, f16[144,1024]{1,0:T(8,128)(2,1)S(1)}, u32[]{:S(2)}, u32[]{:S(2)}) %collective-permute-start.2) | collective-permute-done | bytes 294944 | tf_op jit(solution)/shard_map/ppermute | solution.py:347
  69.9 3.3 %collective-permute-start.3 = (f16[144,1024]{1,0:T(8,128)(2,1)S(1)}, f16[144,1024]{1,0:T(8,128)(2,1)S(1)}, u32[]{:S(2)}, u32[]{:S(2)}) collective-permute-start(f16[144,1024]{1,0:T(8,128)(2,1)S(1)} %add_convert_fusion.9), channel_id=1, source_target_pairs={{0,224},{32,0},{64,32},{96,64},{128,96},{160,128},{192,160},{224,1... | collective-permute-start | bytes 884744 | tf_op jit(solution)/shard_map/ppermute | solution.py:347
  73.6 2.7 %collective-permute-start.10 = (f16[144,1024]{1,0:T(8,128)(2,1)S(1)}, f16[144,1024]{1,0:T(8,128)(2,1)S(1)}, u32[]{:S(2)}, u32[]{:S(2)}) collective-permute-start(f16[144,1024]{1,0:T(8,128)(2,1)S(1)} %add_convert_fusion.4), channel_id=1, source_target_pairs={{0,224},{32,0},{64,32},{96,64},{128,96},{160,128},{192,160},{224,1... | collective-permute-start | bytes 884744 | tf_op jit(solution)/shard_map/ppermute | solution.py:347
  76.3 1.8 %collective-permute-done.3 = f16[144,1024]{1,0:T(8,128)(2,1)S(1)} collective-permute-done((f16[144,1024]{1,0:T(8,128)(2,1)S(1)}, f16[144,1024]{1,0:T(8,128)(2,1)S(1)}, u32[]{:S(2)}, u32[]{:S(2)}) %collective-permute-start.3) | collective-permute-done | bytes 294944 | tf_op jit(solution)/shard_map/ppermute | solution.py:347
  78.2 3.5 %collective-permute-start.4 = (f16[144,1024]{1,0:T(8,128)(2,1)S(1)}, f16[144,1024]{1,0:T(8,128)(2,1)S(1)}, u32[]{:S(2)}, u32[]{:S(2)}) collective-permute-start(f16[144,1024]{1,0:T(8,128)(2,1)S(1)} %add_convert_fusion.8), channel_id=1, source_target_pairs={{0,224},{32,0},{64,32},{96,64},{128,96},{160,128},{192,160},{224,1... | collective-permute-start | bytes 884744 | tf_op jit(solution)/shard_map/ppermute | solution.py:347
  81.7 0.3 collective-permute-done.7
  82.1 0.6 collective-permute-start.8
  82.8 0.4 collective-permute-start.14
  83.2 1.3 collective-permute-done.10
  84.5 3.5 %collective-permute-start.11 = (f16[144,1024]{1,0:T(8,128)(2,1)S(1)}, f16[144,1024]{1,0:T(8,128)(2,1)S(1)}, u32[]{:S(2)}, u32[]{:S(2)}) collective-permute-start(f16[144,1024]{1,0:T(8,128)(2,1)S(1)} %add_convert_fusion.3), channel_id=1, source_target_pairs={{0,224},{32,0},{64,32},{96,64},{128,96},{160,128},{192,160},{224,1... | collective-permute-start | bytes 884744 | tf_op jit(solution)/shard_map/ppermute | solution.py:347
  88.0 2.7 %collective-permute-done.4 = f16[144,1024]{1,0:T(8,128)(2,1)S(1)} collective-permute-done((f16[144,1024]{1,0:T(8,128)(2,1)S(1)}, f16[144,1024]{1,0:T(8,128)(2,1)S(1)}, u32[]{:S(2)}, u32[]{:S(2)}) %collective-permute-start.4) | collective-permute-done | bytes 294944 | tf_op jit(solution)/shard_map/ppermute | solution.py:347
  90.8 3.5 %collective-permute-start.5 = (f16[144,1024]{1,0:T(8,128)(2,1)S(1)}, f16[144,1024]{1,0:T(8,128)(2,1)S(1)}, u32[]{:S(2)}, u32[]{:S(2)}) collective-permute-start(f16[144,1024]{1,0:T(8,128)(2,1)S(1)} %add_convert_fusion.7), channel_id=1, source_target_pairs={{0,224},{32,0},{64,32},{96,64},{128,96},{160,128},{192,160},{224,1... | collective-permute-start | bytes 884744 | tf_op jit(solution)/shard_map/ppermute | solution.py:347
  94.5 2.5 %collective-permute-done.11 = f16[144,1024]{1,0:T(8,128)(2,1)S(1)} collective-permute-done((f16[144,1024]{1,0:T(8,128)(2,1)S(1)}, f16[144,1024]{1,0:T(8,128)(2,1)S(1)}, u32[]{:S(2)}, u32[]{:S(2)}) %collective-permute-start.11) | collective-permute-done | bytes 294944 | tf_op jit(solution)/shard_map/ppermute | solution.py:347
  97.1 6.3 %collective-permute-done.5 = f16[144,1024]{1,0:T(8,128)(2,1)S(1)} collective-permute-done((f16[144,1024]{1,0:T(8,128)(2,1)S(1)}, f16[144,1024]{1,0:T(8,128)(2,1)S(1)}, u32[]{:S(2)}, u32[]{:S(2)}) %collective-permute-start.5) | collective-permute-done | bytes 294944 | tf_op jit(solution)/shard_map/ppermute | solution.py:347
  103.4 0.4 multiply_convert_fusion
  103.9 3.5 %collective-permute-start.16 = (bf16[144,512]{1,0:T(8,128)(2,1)S(1)}, bf16[144,512]{1,0:T(8,128)(2,1)S(1)}, u32[]{:S(2)}, u32[]{:S(2)}) collective-permute-start(bf16[144,512]{1,0:T(8,128)(2,1)S(1)} %get-tuple-element.60.refs_2_), channel_id=1, source_target_pairs={{0,224},{32,0},{64,32},{96,64},{128,96},{160,128},{192,160},{224,1... | collective-permute-start | bytes 442376 | tf_op jit(solution)/shard_map/ppermute | solution.py:380
  107.4 1.4 collective-permute-start.19
  108.9 1.0 collective-permute-done.25.refs_5_
  109.8 2.8 %collective-permute-start.17 = (bf16[144,512]{1,0:T(8,128)(2,1)S(1)}, bf16[144,512]{1,0:T(8,128)(2,1)S(1)}, u32[]{:S(2)}, u32[]{:S(2)}) collective-permute-start(bf16[144,512]{1,0:T(8,128)(2,1)S(1)} %collective-permute-done.16.refs_0_), channel_id=1, source_target_pairs={{0,224},{32,0},{64,32},{96,64},{128,96},{160,128},{192,160},{224,1... | collective-permute-start | bytes 442376 | tf_op jit(solution)/shard_map/ppermute | solution.py:380
  112.6 1.6 collective-permute-start.20
  114.2 1.6 collective-permute-done.22.refs_4_
  115.8 2.7 %collective-permute-done.26.refs_7_ = bf16[144,512]{1,0:T(8,128)(2,1)S(1)} collective-permute-done((bf16[144,512]{1,0:T(8,128)(2,1)S(1)}, bf16[144,512]{1,0:T(8,128)(2,1)S(1)}, u32[]{:S(2)}, u32[]{:S(2)}) %collective-permute-start.26) | collective-permute-done | bytes 147488 | tf_op jit(solution)/shard_map/ppermute | solution.py:381
  118.5 2.7 %collective-permute-start.18 = (bf16[144,512]{1,0:T(8,128)(2,1)S(1)}, bf16[144,512]{1,0:T(8,128)(2,1)S(1)}, u32[]{:S(2)}, u32[]{:S(2)}) collective-permute-start(bf16[144,512]{1,0:T(8,128)(2,1)S(1)} %collective-permute-done.17.refs_2_), channel_id=1, source_target_pairs={{0,224},{32,0},{64,32},{96,64},{128,96},{160,128},{192,160},{224,1... | collective-permute-start | bytes 442376 | tf_op jit(solution)/shard_map/ppermute | solution.py:380
  121.2 0.6 collective-permute-start.21
  121.7 0.1 collective-permute-done.23.refs_6_
  121.9 0.8 collective-permute-start.24
  122.6 1.5 collective-permute-done.27.refs_5_
  124.2 3.4 %collective-permute-start.28 = (bf16[144,512]{1,0:T(8,128)(2,1)S(1)}, bf16[144,512]{1,0:T(8,128)(2,1)S(1)}, u32[]{:S(2)}, u32[]{:S(2)}) collective-permute-start(bf16[144,512]{1,0:T(8,128)(2,1)S(1)} %collective-permute-done.18.refs_0_), channel_id=1, source_target_pairs={{0,224},{32,0},{64,32},{96,64},{128,96},{160,128},{192,160},{224,1... | collective-permute-start | bytes 442376 | tf_op jit(solution)/shard_map/ppermute | solution.py:380
  127.6 1.7 down_dots.3
  129.3 8.2 %collective-permute-start.31 = (f32[2,144,896]{2,1,0:T(8,128)S(1)}, f32[2,144,896]{2,1,0:T(8,128)S(1)}, u32[]{:S(2)}, u32[]{:S(2)}) collective-permute-start(f32[2,144,896]{2,1,0:T(8,128)S(1)} %get-tuple-element.54), channel_id=1, source_target_pairs={{0,1},{1,0},{2,3},{3,2},{4,5},{5,4},{6,7},{7,6},{8,9},{9,8},{10,11... | collective-permute-start | bytes 3096584 | tf_op jit(solution)/shard_map/ppermute | solution.py:391
  137.5 1.7 down_dots.2
  139.2 1.4 collective-permute-start.30
  140.6 0.1 settle.2
  140.7 2.2 %collective-permute-done.30.came_ref = f32[2,144,896]{2,1,0:T(8,128)S(1)} collective-permute-done((f32[2,144,896]{2,1,0:T(8,128)S(1)}, f32[2,144,896]{2,1,0:T(8,128)S(1)}, u32[]{:S(2)}, u32[]{:S(2)}) %collective-permute-start.30) | collective-permute-done | bytes 1032224 | tf_op jit(solution)/shard_map/ppermute | solution.py:391
  142.9 1.1 settle.3
  144.0 3.6 %all-to-all-start.2 = ((bf16[16,32,896]{2,1,0:T(8,128)(2,1)}), bf16[16,32,896]{2,1,0:T(8,128)(2,1)S(1)}, u32[]{:S(2)}, u32[]{:S(2)}) async-start(bf16[16,32,896]{2,1,0:T(8,128)(2,1)} %get-tuple-element.56), calls=%async_computation.2 | async-start | bytes 1835008 | tf_op jit(solution)/shard_map/all_to_all | solution.py:394
  147.6 15.1 %all-to-all-done.2 = bf16[16,32,896]{2,1,0:T(8,128)(2,1)S(1)} async-done(((bf16[16,32,896]{2,1,0:T(8,128)(2,1)}), bf16[16,32,896]{2,1,0:T(8,128)(2,1)S(1)}, u32[]{:S(2)}, u32[]{:S(2)}) %all-to-all-start.2) | async-done | bytes 917536 | tf_op jit(solution)/shard_map/all_to_all | solution.py:394
  162.7 1.6 combine.1
  164.4 3.0 %collective-permute-start.32 = (bf16[16,896]{1,0:T(8,128)(2,1)S(1)}, bf16[16,896]{1,0:T(8,128)(2,1)S(1)}, u32[]{:S(2)}, u32[]{:S(2)}) collective-permute-start(bf16[16,896]{1,0:T(8,128)(2,1)S(1)} %get-tuple-element.64), channel_id=1, source_target_pairs={{0,32},{1,225},{32,64},{33,1},{64,96},{65,33},{96,128},{97,65},{12... | collective-permute-start | bytes 86024 | tf_op jit(solution)/shard_map/ppermute | solution.py:399
  167.4 2.7 %collective-permute-start.35 = (bf16[16,896]{1,0:T(8,128)(2,1)S(1)}, bf16[16,896]{1,0:T(8,128)(2,1)S(1)}, u32[]{:S(2)}, u32[]{:S(2)}) collective-permute-start(bf16[16,896]{1,0:T(8,128)(2,1)S(1)} %get-tuple-element.61), channel_id=1, source_target_pairs={{0,0},{1,129},{32,32},{33,161},{64,64},{65,193},{96,96},{97,225},{... | collective-permute-start | bytes 86024 | tf_op jit(solution)/shard_map/ppermute | solution.py:399
  170.1 2.0 %collective-permute-start.34 = (bf16[16,896]{1,0:T(8,128)(2,1)S(1)}, bf16[16,896]{1,0:T(8,128)(2,1)S(1)}, u32[]{:S(2)}, u32[]{:S(2)}) collective-permute-start(bf16[16,896]{1,0:T(8,128)(2,1)S(1)} %get-tuple-element.62), channel_id=1, source_target_pairs={{0,96},{1,161},{32,128},{33,193},{64,160},{65,225},{96,192},{97,1}... | collective-permute-start | bytes 86024 | tf_op jit(solution)/shard_map/ppermute | solution.py:399
  172.1 2.7 %collective-permute-start.33 = (bf16[16,896]{1,0:T(8,128)(2,1)S(1)}, bf16[16,896]{1,0:T(8,128)(2,1)S(1)}, u32[]{:S(2)}, u32[]{:S(2)}) collective-permute-start(bf16[16,896]{1,0:T(8,128)(2,1)S(1)} %get-tuple-element.63), channel_id=1, source_target_pairs={{0,64},{1,193},{32,96},{33,225},{64,128},{65,1},{96,160},{97,33},{... | collective-permute-start | bytes 86024 | tf_op jit(solution)/shard_map/ppermute | solution.py:399
  174.8 1.0 collective-permute-done.33
  175.8 0.1 collective-permute-done.35
  175.9 1.3 collective-permute-done.36.refs_1_
  177.3 1.3 assemble.1
  (75 shorter events, 1.9 us)
Async XLA Ops:
  0.0 0.9 copy-start.7
  0.9 0.7 copy-start.8
  1.6 0.7 copy-start.9
  3.5 16.8 %all-to-all-start = ((bf16[8,12,512]{2,1,0:T(8,128)(2,1)}), bf16[8,12,512]{2,1,0:T(8,128)(2,1)S(1)}, u32[]{:S(2)}, u32[]{:S(2)}) async-start(bf16[8,12,512]{2,1,0:T(8,128)(2,1)} %prep.1), calls=%async_computation | async-start | bytes 262144 | tf_op jit(solution)/shard_map/all_to_all | solution.py:356
  21.6 27.4 %copy-start.4 = (bf16[896,1024]{1,0:T(8,128)(2,1)S(1)}, bf16[896,1024]{1,0:T(8,128)(2,1)}, u32[]{:S(2)}) copy-start(bf16[896,1024]{1,0:T(8,128)(2,1)} %sg_ref.3) | copy-start | bytes 5505028
  43.2 5.6 %collective-permute-start = (bf16[16,64,448]{2,1,0:T(8,128)(2,1)S(1)}, bf16[16,64,448]{2,1,0:T(8,128)(2,1)S(1)}, u32[]{:S(2)}, u32[]{:S(2)}) collective-permute-start(bf16[16,64,448]{2,1,0:T(8,128)(2,1)S(1)} %all_to_all.15), channel_id=1, source_target_pairs={{0,1},{1,0},{2,3},{3,2},{4,5},{5,4},{6,7},{7,6},{8,9},{9,8},{10,11... | collective-permute-start | bytes 2752520 | tf_op jit(solution)/shard_map/ppermute | solution.py:360
  46.5 2.5 %copy-start.2 = (bf16[1,896,1024]{2,1,0:T(8,128)(2,1)S(1)}, bf16[1,896,1024]{2,1,0:T(8,128)(2,1)}, u32[]{:S(2)}) copy-start(bf16[1,896,1024]{2,1,0:T(8,128)(2,1)} %wg_ref.3) | copy-start | bytes 5505028
  46.5 2.5 %copy-start.3 = (bf16[1,896,1024]{2,1,0:T(8,128)(2,1)S(1)}, bf16[1,896,1024]{2,1,0:T(8,128)(2,1)}, u32[]{:S(2)}) copy-start(bf16[1,896,1024]{2,1,0:T(8,128)(2,1)} %wu_ref.3) | copy-start | bytes 5505028
  46.5 2.5 %collective-permute-start.1 = (bf16[128,448]{1,0:T(8,128)(2,1)S(1)}, bf16[128,448]{1,0:T(8,128)(2,1)S(1)}, u32[]{:S(2)}, u32[]{:S(2)}) collective-permute-start(bf16[128,448]{1,0:T(8,128)(2,1)S(1)} %get-tuple-element.34.so_ref), channel_id=1, source_target_pairs={{0,1},{1,0},{2,3},{3,2},{4,5},{5,4},{6,7},{7,6},{8,9},{9,8},{10,11... | collective-permute-start | bytes 344072 | tf_op jit(solution)/shard_map/ppermute | solution.py:358
  49.0 1.5 copy-start.5
  54.6 5.7 %copy-start.6 = (bf16[896,1024]{1,0:T(8,128)(2,1)S(1)}, bf16[896,1024]{1,0:T(8,128)(2,1)}, u32[]{:S(2)}) copy-start(bf16[896,1024]{1,0:T(8,128)(2,1)} %su_ref.3) | copy-start | bytes 5505028
  54.7 11.1 %collective-permute-start.12 = (f16[144,1024]{1,0:T(8,128)(2,1)S(1)}, f16[144,1024]{1,0:T(8,128)(2,1)S(1)}, u32[]{:S(2)}, u32[]{:S(2)}) collective-permute-start(f16[144,1024]{1,0:T(8,128)(2,1)S(1)} %convert_element_type.107), channel_id=1, source_target_pairs={{0,32},{32,64},{64,96},{96,128},{128,160},{160,192},{192,224},{224... | collective-permute-start | bytes 884744 | tf_op jit(solution)/shard_map/ppermute | solution.py:347
  55.5 17.9 %collective-permute-start.9 = (f16[144,1024]{1,0:T(8,128)(2,1)S(1)}, f16[144,1024]{1,0:T(8,128)(2,1)S(1)}, u32[]{:S(2)}, u32[]{:S(2)}) collective-permute-start(f16[144,1024]{1,0:T(8,128)(2,1)S(1)} %convert_element_type.101), channel_id=1, source_target_pairs={{0,224},{32,0},{64,32},{96,64},{128,96},{160,128},{192,160},{224,1... | collective-permute-start | bytes 884744 | tf_op jit(solution)/shard_map/ppermute | solution.py:347
  57.7 15.6 %collective-permute-start.6 = (f16[144,1024]{1,0:T(8,128)(2,1)S(1)}, f16[144,1024]{1,0:T(8,128)(2,1)S(1)}, u32[]{:S(2)}, u32[]{:S(2)}) collective-permute-start(f16[144,1024]{1,0:T(8,128)(2,1)S(1)} %convert_element_type.95), channel_id=1, source_target_pairs={{0,32},{32,64},{64,96},{96,128},{128,160},{160,192},{192,224},{224... | collective-permute-start | bytes 884744 | tf_op jit(solution)/shard_map/ppermute | solution.py:347
  57.7 12.2 %collective-permute-start.2 = (f16[144,1024]{1,0:T(8,128)(2,1)S(1)}, f16[144,1024]{1,0:T(8,128)(2,1)S(1)}, u32[]{:S(2)}, u32[]{:S(2)}) collective-permute-start(f16[144,1024]{1,0:T(8,128)(2,1)S(1)} %convert_element_type.87), channel_id=1, source_target_pairs={{0,224},{32,0},{64,32},{96,64},{128,96},{160,128},{192,160},{224,1... | collective-permute-start | bytes 884744 | tf_op jit(solution)/shard_map/ppermute | solution.py:347
  65.9 16.8 %collective-permute-start.13 = (f16[144,1024]{1,0:T(8,128)(2,1)S(1)}, f16[144,1024]{1,0:T(8,128)(2,1)S(1)}, u32[]{:S(2)}, u32[]{:S(2)}) collective-permute-start(f16[144,1024]{1,0:T(8,128)(2,1)S(1)} %add_convert_fusion.2), channel_id=1, source_target_pairs={{0,32},{32,64},{64,96},{96,128},{128,160},{160,192},{192,224},{224... | collective-permute-start | bytes 884744 | tf_op jit(solution)/shard_map/ppermute | solution.py:347
  69.9 8.2 %collective-permute-start.3 = (f16[144,1024]{1,0:T(8,128)(2,1)S(1)}, f16[144,1024]{1,0:T(8,128)(2,1)S(1)}, u32[]{:S(2)}, u32[]{:S(2)}) collective-permute-start(f16[144,1024]{1,0:T(8,128)(2,1)S(1)} %add_convert_fusion.9), channel_id=1, source_target_pairs={{0,224},{32,0},{64,32},{96,64},{128,96},{160,128},{192,160},{224,1... | collective-permute-start | bytes 884744 | tf_op jit(solution)/shard_map/ppermute | solution.py:347
  73.4 8.6 %collective-permute-start.7 = (f16[144,1024]{1,0:T(8,128)(2,1)S(1)}, f16[144,1024]{1,0:T(8,128)(2,1)S(1)}, u32[]{:S(2)}, u32[]{:S(2)}) collective-permute-start(f16[144,1024]{1,0:T(8,128)(2,1)S(1)} %add_convert_fusion.6), channel_id=1, source_target_pairs={{0,32},{32,64},{64,96},{96,128},{128,160},{160,192},{192,224},{224... | collective-permute-start | bytes 884744 | tf_op jit(solution)/shard_map/ppermute | solution.py:347
  73.6 10.9 %collective-permute-start.10 = (f16[144,1024]{1,0:T(8,128)(2,1)S(1)}, f16[144,1024]{1,0:T(8,128)(2,1)S(1)}, u32[]{:S(2)}, u32[]{:S(2)}) collective-permute-start(f16[144,1024]{1,0:T(8,128)(2,1)S(1)} %add_convert_fusion.4), channel_id=1, source_target_pairs={{0,224},{32,0},{64,32},{96,64},{128,96},{160,128},{192,160},{224,1... | collective-permute-start | bytes 884744 | tf_op jit(solution)/shard_map/ppermute | solution.py:347
  78.2 12.6 %collective-permute-start.4 = (f16[144,1024]{1,0:T(8,128)(2,1)S(1)}, f16[144,1024]{1,0:T(8,128)(2,1)S(1)}, u32[]{:S(2)}, u32[]{:S(2)}) collective-permute-start(f16[144,1024]{1,0:T(8,128)(2,1)S(1)} %add_convert_fusion.8), channel_id=1, source_target_pairs={{0,224},{32,0},{64,32},{96,64},{128,96},{160,128},{192,160},{224,1... | collective-permute-start | bytes 884744 | tf_op jit(solution)/shard_map/ppermute | solution.py:347
  82.1 12.4 %collective-permute-start.8 = (f16[144,1024]{1,0:T(8,128)(2,1)S(1)}, f16[144,1024]{1,0:T(8,128)(2,1)S(1)}, u32[]{:S(2)}, u32[]{:S(2)}) collective-permute-start(f16[144,1024]{1,0:T(8,128)(2,1)S(1)} %add_convert_fusion.5), channel_id=1, source_target_pairs={{0,32},{32,64},{64,96},{96,128},{128,160},{160,192},{192,224},{224... | collective-permute-start | bytes 884744 | tf_op jit(solution)/shard_map/ppermute | solution.py:347
  82.8 11.5 %collective-permute-start.14 = (f16[144,1024]{1,0:T(8,128)(2,1)S(1)}, f16[144,1024]{1,0:T(8,128)(2,1)S(1)}, u32[]{:S(2)}, u32[]{:S(2)}) collective-permute-start(f16[144,1024]{1,0:T(8,128)(2,1)S(1)} %add_convert_fusion.1), channel_id=1, source_target_pairs={{0,32},{32,64},{64,96},{96,128},{128,160},{160,192},{192,224},{224... | collective-permute-start | bytes 884744 | tf_op jit(solution)/shard_map/ppermute | solution.py:347
  84.5 12.6 %collective-permute-start.11 = (f16[144,1024]{1,0:T(8,128)(2,1)S(1)}, f16[144,1024]{1,0:T(8,128)(2,1)S(1)}, u32[]{:S(2)}, u32[]{:S(2)}) collective-permute-start(f16[144,1024]{1,0:T(8,128)(2,1)S(1)} %add_convert_fusion.3), channel_id=1, source_target_pairs={{0,224},{32,0},{64,32},{96,64},{128,96},{160,128},{192,160},{224,1... | collective-permute-start | bytes 884744 | tf_op jit(solution)/shard_map/ppermute | solution.py:347
  90.8 12.6 %collective-permute-start.5 = (f16[144,1024]{1,0:T(8,128)(2,1)S(1)}, f16[144,1024]{1,0:T(8,128)(2,1)S(1)}, u32[]{:S(2)}, u32[]{:S(2)}) collective-permute-start(f16[144,1024]{1,0:T(8,128)(2,1)S(1)} %add_convert_fusion.7), channel_id=1, source_target_pairs={{0,224},{32,0},{64,32},{96,64},{128,96},{160,128},{192,160},{224,1... | collective-permute-start | bytes 884744 | tf_op jit(solution)/shard_map/ppermute | solution.py:347
  94.3 33.3 %copy-start.1 = (bf16[1024,896]{1,0:T(8,128)(2,1)S(1)}, bf16[1024,896]{1,0:T(8,128)(2,1)}, u32[]{:S(2)}) copy-start(bf16[1024,896]{1,0:T(8,128)(2,1)} %refs_9_.3) | copy-start | bytes 5505028
  94.4 33.2 %copy-start = (bf16[1,1024,896]{2,1,0:T(8,128)(2,1)S(1)}, bf16[1,1024,896]{2,1,0:T(8,128)(2,1)}, u32[]{:S(2)}) copy-start(bf16[1,1024,896]{2,1,0:T(8,128)(2,1)} %refs_8_.3) | copy-start | bytes 5505028
  94.4 9.0 %collective-permute-start.15 = (f16[144,1024]{1,0:T(8,128)(2,1)S(1)}, f16[144,1024]{1,0:T(8,128)(2,1)S(1)}, u32[]{:S(2)}, u32[]{:S(2)}) collective-permute-start(f16[144,1024]{1,0:T(8,128)(2,1)S(1)} %add_convert_fusion), channel_id=1, source_target_pairs={{0,32},{32,64},{64,96},{96,128},{128,160},{160,192},{192,224},{224... | collective-permute-start | bytes 884744 | tf_op jit(solution)/shard_map/ppermute | solution.py:347
  103.8 6.0 %collective-permute-start.25 = (bf16[144,512]{1,0:T(8,128)(2,1)S(1)}, bf16[144,512]{1,0:T(8,128)(2,1)S(1)}, u32[]{:S(2)}, u32[]{:S(2)}) collective-permute-start(bf16[144,512]{1,0:T(8,128)(2,1)S(1)} %get-tuple-element.59.refs_3_), channel_id=1, source_target_pairs={{0,32},{32,64},{64,96},{96,128},{128,160},{160,192},{192,224},{224... | collective-permute-start | bytes 442376 | tf_op jit(solution)/shard_map/ppermute | solution.py:381
  103.9 5.9 %collective-permute-start.16 = (bf16[144,512]{1,0:T(8,128)(2,1)S(1)}, bf16[144,512]{1,0:T(8,128)(2,1)S(1)}, u32[]{:S(2)}, u32[]{:S(2)}) collective-permute-start(bf16[144,512]{1,0:T(8,128)(2,1)S(1)} %get-tuple-element.60.refs_2_), channel_id=1, source_target_pairs={{0,224},{32,0},{64,32},{96,64},{128,96},{160,128},{192,160},{224,1... | collective-permute-start | bytes 442376 | tf_op jit(solution)/shard_map/ppermute | solution.py:380
  107.4 5.2 %collective-permute-start.19 = (bf16[144,512]{1,0:T(8,128)(2,1)S(1)}, bf16[144,512]{1,0:T(8,128)(2,1)S(1)}, u32[]{:S(2)}, u32[]{:S(2)}) collective-permute-start(bf16[144,512]{1,0:T(8,128)(2,1)S(1)} %get-tuple-element.59.refs_3_), channel_id=1, source_target_pairs={{0,224},{32,0},{64,32},{96,64},{128,96},{160,128},{192,160},{224,1... | collective-permute-start | bytes 442376 | tf_op jit(solution)/shard_map/ppermute | solution.py:383
  108.8 7.0 %collective-permute-start.22 = (bf16[144,512]{1,0:T(8,128)(2,1)S(1)}, bf16[144,512]{1,0:T(8,128)(2,1)S(1)}, u32[]{:S(2)}, u32[]{:S(2)}) collective-permute-start(bf16[144,512]{1,0:T(8,128)(2,1)S(1)} %get-tuple-element.60.refs_2_), channel_id=1, source_target_pairs={{0,32},{32,64},{64,96},{96,128},{128,160},{160,192},{192,224},{224... | collective-permute-start | bytes 442376 | tf_op jit(solution)/shard_map/ppermute | solution.py:384
  109.8 8.7 %collective-permute-start.26 = (bf16[144,512]{1,0:T(8,128)(2,1)S(1)}, bf16[144,512]{1,0:T(8,128)(2,1)S(1)}, u32[]{:S(2)}, u32[]{:S(2)}) collective-permute-start(bf16[144,512]{1,0:T(8,128)(2,1)S(1)} %collective-permute-done.25.refs_5_), channel_id=1, source_target_pairs={{0,32},{32,64},{64,96},{96,128},{128,160},{160,192},{192,224},{224... | collective-permute-start | bytes 442376 | tf_op jit(solution)/shard_map/ppermute | solution.py:381
  109.8 8.7 %collective-permute-start.17 = (bf16[144,512]{1,0:T(8,128)(2,1)S(1)}, bf16[144,512]{1,0:T(8,128)(2,1)S(1)}, u32[]{:S(2)}, u32[]{:S(2)}) collective-permute-start(bf16[144,512]{1,0:T(8,128)(2,1)S(1)} %collective-permute-done.16.refs_0_), channel_id=1, source_target_pairs={{0,224},{32,0},{64,32},{96,64},{128,96},{160,128},{192,160},{224,1... | collective-permute-start | bytes 442376 | tf_op jit(solution)/shard_map/ppermute | solution.py:380
  112.6 8.6 %collective-permute-start.20 = (bf16[144,512]{1,0:T(8,128)(2,1)S(1)}, bf16[144,512]{1,0:T(8,128)(2,1)S(1)}, u32[]{:S(2)}, u32[]{:S(2)}) collective-permute-start(bf16[144,512]{1,0:T(8,128)(2,1)S(1)} %collective-permute-done.19.refs_1_), channel_id=1, source_target_pairs={{0,224},{32,0},{64,32},{96,64},{128,96},{160,128},{192,160},{224,1... | collective-permute-start | bytes 442376 | tf_op jit(solution)/shard_map/ppermute | solution.py:383
  115.8 6.1 %collective-permute-start.23 = (bf16[144,512]{1,0:T(8,128)(2,1)S(1)}, bf16[144,512]{1,0:T(8,128)(2,1)S(1)}, u32[]{:S(2)}, u32[]{:S(2)}) collective-permute-start(bf16[144,512]{1,0:T(8,128)(2,1)S(1)} %collective-permute-done.22.refs_4_), channel_id=1, source_target_pairs={{0,32},{32,64},{64,96},{96,128},{128,160},{160,192},{192,224},{224... | collective-permute-start | bytes 442376 | tf_op jit(solution)/shard_map/ppermute | solution.py:384
  118.5 5.6 %collective-permute-start.27 = (bf16[144,512]{1,0:T(8,128)(2,1)S(1)}, bf16[144,512]{1,0:T(8,128)(2,1)S(1)}, u32[]{:S(2)}, u32[]{:S(2)}) collective-permute-start(bf16[144,512]{1,0:T(8,128)(2,1)S(1)} %collective-permute-done.26.refs_7_), channel_id=1, source_target_pairs={{0,32},{32,64},{64,96},{96,128},{128,160},{160,192},{192,224},{224... | collective-permute-start | bytes 442376 | tf_op jit(solution)/shard_map/ppermute | solution.py:381
  118.5 5.7 %collective-permute-start.18 = (bf16[144,512]{1,0:T(8,128)(2,1)S(1)}, bf16[144,512]{1,0:T(8,128)(2,1)S(1)}, u32[]{:S(2)}, u32[]{:S(2)}) collective-permute-start(bf16[144,512]{1,0:T(8,128)(2,1)S(1)} %collective-permute-done.17.refs_2_), channel_id=1, source_target_pairs={{0,224},{32,0},{64,32},{96,64},{128,96},{160,128},{192,160},{224,1... | collective-permute-start | bytes 442376 | tf_op jit(solution)/shard_map/ppermute | solution.py:380
  121.2 16.3 %collective-permute-start.21 = (bf16[144,512]{1,0:T(8,128)(2,1)S(1)}, bf16[144,512]{1,0:T(8,128)(2,1)S(1)}, u32[]{:S(2)}, u32[]{:S(2)}) collective-permute-start(bf16[144,512]{1,0:T(8,128)(2,1)S(1)} %collective-permute-done.20.refs_3_), channel_id=1, source_target_pairs={{0,224},{32,0},{64,32},{96,64},{128,96},{160,128},{192,160},{224,1... | collective-permute-start | bytes 442376 | tf_op jit(solution)/shard_map/ppermute | solution.py:383
  121.9 15.6 %collective-permute-start.24 = (bf16[144,512]{1,0:T(8,128)(2,1)S(1)}, bf16[144,512]{1,0:T(8,128)(2,1)S(1)}, u32[]{:S(2)}, u32[]{:S(2)}) collective-permute-start(bf16[144,512]{1,0:T(8,128)(2,1)S(1)} %collective-permute-done.23.refs_6_), channel_id=1, source_target_pairs={{0,32},{32,64},{64,96},{96,128},{128,160},{160,192},{192,224},{224... | collective-permute-start | bytes 442376 | tf_op jit(solution)/shard_map/ppermute | solution.py:384
  124.1 13.4 %collective-permute-start.29 = (bf16[144,512]{1,0:T(8,128)(2,1)S(1)}, bf16[144,512]{1,0:T(8,128)(2,1)S(1)}, u32[]{:S(2)}, u32[]{:S(2)}) collective-permute-start(bf16[144,512]{1,0:T(8,128)(2,1)S(1)} %collective-permute-done.27.refs_5_), channel_id=1, source_target_pairs={{0,32},{32,64},{64,96},{96,128},{128,160},{160,192},{192,224},{224... | collective-permute-start | bytes 442376 | tf_op jit(solution)/shard_map/ppermute | solution.py:381
  124.2 13.3 %collective-permute-start.28 = (bf16[144,512]{1,0:T(8,128)(2,1)S(1)}, bf16[144,512]{1,0:T(8,128)(2,1)S(1)}, u32[]{:S(2)}, u32[]{:S(2)}) collective-permute-start(bf16[144,512]{1,0:T(8,128)(2,1)S(1)} %collective-permute-done.18.refs_0_), channel_id=1, source_target_pairs={{0,224},{32,0},{64,32},{96,64},{128,96},{160,128},{192,160},{224,1... | collective-permute-start | bytes 442376 | tf_op jit(solution)/shard_map/ppermute | solution.py:380
  129.3 11.3 %collective-permute-start.31 = (f32[2,144,896]{2,1,0:T(8,128)S(1)}, f32[2,144,896]{2,1,0:T(8,128)S(1)}, u32[]{:S(2)}, u32[]{:S(2)}) collective-permute-start(f32[2,144,896]{2,1,0:T(8,128)S(1)} %get-tuple-element.54), channel_id=1, source_target_pairs={{0,1},{1,0},{2,3},{3,2},{4,5},{5,4},{6,7},{7,6},{8,9},{9,8},{10,11... | collective-permute-start | bytes 3096584 | tf_op jit(solution)/shard_map/ppermute | solution.py:391
  139.2 3.7 %collective-permute-start.30 = (f32[2,144,896]{2,1,0:T(8,128)S(1)}, f32[2,144,896]{2,1,0:T(8,128)S(1)}, u32[]{:S(2)}, u32[]{:S(2)}) collective-permute-start(f32[2,144,896]{2,1,0:T(8,128)S(1)} %get-tuple-element.52), channel_id=1, source_target_pairs={{0,1},{1,0},{2,3},{3,2},{4,5},{5,4},{6,7},{7,6},{8,9},{9,8},{10,11... | collective-permute-start | bytes 3096584 | tf_op jit(solution)/shard_map/ppermute | solution.py:391
  142.9 4.7 %copy-start.10 = (s32[4]{0:T(128)S(1)}, s32[4]{0:T(128)}, u32[]{:S(2)}) copy-start(s32[4]{0:T(128)} %constant.36.clone) | copy-start | bytes 52
  142.9 4.7 %copy-start.11 = (s32[4]{0:T(128)S(1)}, s32[4]{0:T(128)}, u32[]{:S(2)}) copy-start(s32[4]{0:T(128)} %constant.35.clone) | copy-start | bytes 52
  144.0 18.8 %all-to-all-start.2 = ((bf16[16,32,896]{2,1,0:T(8,128)(2,1)}), bf16[16,32,896]{2,1,0:T(8,128)(2,1)S(1)}, u32[]{:S(2)}, u32[]{:S(2)}) async-start(bf16[16,32,896]{2,1,0:T(8,128)(2,1)} %get-tuple-element.56), calls=%async_computation.2 | async-start | bytes 1835008 | tf_op jit(solution)/shard_map/all_to_all | solution.py:394
  164.4 10.4 %collective-permute-start.32 = (bf16[16,896]{1,0:T(8,128)(2,1)S(1)}, bf16[16,896]{1,0:T(8,128)(2,1)S(1)}, u32[]{:S(2)}, u32[]{:S(2)}) collective-permute-start(bf16[16,896]{1,0:T(8,128)(2,1)S(1)} %get-tuple-element.64), channel_id=1, source_target_pairs={{0,32},{1,225},{32,64},{33,1},{64,96},{65,33},{96,128},{97,65},{12... | collective-permute-start | bytes 86024 | tf_op jit(solution)/shard_map/ppermute | solution.py:399
  167.4 8.5 %collective-permute-start.35 = (bf16[16,896]{1,0:T(8,128)(2,1)S(1)}, bf16[16,896]{1,0:T(8,128)(2,1)S(1)}, u32[]{:S(2)}, u32[]{:S(2)}) collective-permute-start(bf16[16,896]{1,0:T(8,128)(2,1)S(1)} %get-tuple-element.61), channel_id=1, source_target_pairs={{0,0},{1,129},{32,32},{33,161},{64,64},{65,193},{96,96},{97,225},{... | collective-permute-start | bytes 86024 | tf_op jit(solution)/shard_map/ppermute | solution.py:399
  170.1 5.7 %collective-permute-start.34 = (bf16[16,896]{1,0:T(8,128)(2,1)S(1)}, bf16[16,896]{1,0:T(8,128)(2,1)S(1)}, u32[]{:S(2)}, u32[]{:S(2)}) collective-permute-start(bf16[16,896]{1,0:T(8,128)(2,1)S(1)} %get-tuple-element.62), channel_id=1, source_target_pairs={{0,96},{1,161},{32,128},{33,193},{64,160},{65,225},{96,192},{97,1}... | collective-permute-start | bytes 86024 | tf_op jit(solution)/shard_map/ppermute | solution.py:399
  172.1 3.7 %collective-permute-start.33 = (bf16[16,896]{1,0:T(8,128)(2,1)S(1)}, bf16[16,896]{1,0:T(8,128)(2,1)S(1)}, u32[]{:S(2)}, u32[]{:S(2)}) collective-permute-start(bf16[16,896]{1,0:T(8,128)(2,1)S(1)} %get-tuple-element.63), channel_id=1, source_target_pairs={{0,64},{1,193},{32,96},{33,225},{64,128},{65,1},{96,160},{97,33},{... | collective-permute-start | bytes 86024 | tf_op jit(solution)/shard_map/ppermute | solution.py:399
  175.9 1.3 collective-permute-start.36
